TPU v7x, 32 devices: a whole 2x2x4 slice. The times are simulated.
32 devices in a mesh: gx: 4 (over z), gy: 4 (over y, core), gz: 2 (over x).
Axes of the slice: x: 2, y: 2, z: 4, core: 2. Of those that a mesh axis runs over, the one named last changes fastest.
Arguments:
- right_side: float32 [128, 128, 256], P('gx', 'gy', 'gz'), may hold values from -8 to 8
- guess: float32 [128, 128, 256], P('gx', 'gy', 'gz'), may hold values from -4 to 4
Outputs:
- solution_field: float32 [128, 128, 256], P('gx', 'gy', 'gz')
- residual: float32 [128, 128, 256], P('gx', 'gy', 'gz')
All inputs are finite; a program needn't handle non-finite values.
Results may differ from a plain program's by a relative error of at most 0.0001.
Values sent between devices are 32-bit elements; how exact they have to be, the bound alone decides.
No kernel may reach another device: no remote copies, remote signals or barrier semaphores. Data moves between devices by JAX's collectives and lax.ppermute only.
A program may use at most 128 MiB of HBM per device.

v0:
```python
import jax
import jax.numpy as jnp
from jax import lax
from jax.sharding import PartitionSpec as P

LEVELS = 6
SWEEPS = 4
STEPS = 2


damping = 2.0 / 3.0


def passed_along(value, axis, steps):
    count = lax.axis_size(axis)
    first, last = (max(0, -steps), min(count, count - steps))
    return lax.ppermute(value, axis, [(source, source + steps) for source in range(first, last)])


def padded_2(x, sides, width):
    for axis, dim in sides:
        count, length = (lax.axis_size(axis), x.shape[dim])
        up = [(i, (i + 1) % count) for i in range(count - 1)]
        down = [(j, i) for i, j in up]
        last = lax.slice_in_dim(x, length - width, length, axis=dim)
        first = lax.slice_in_dim(x, 0, width, axis=dim)
        before = lax.ppermute(last, axis, up)
        after = lax.ppermute(first, axis, down)
        x = jnp.concatenate([before, x, after], axis=dim)
    return x


def padded_stencil(padded):
    beside = padded[2:, 1:-1, 1:-1] + padded[:-2, 1:-1, 1:-1]
    beside = beside + padded[1:-1, 2:, 1:-1] + padded[1:-1, :-2, 1:-1]
    beside = beside + padded[1:-1, 1:-1, 2:] + padded[1:-1, 1:-1, :-2]
    return 6.0 * padded[1:-1, 1:-1, 1:-1] - beside


def restrict(field):
    first, second, third = field.shape
    blocks = field.reshape(first // 2, 2, second // 2, 2, third // 2, 2)
    return jnp.mean(blocks, axis=(1, 3, 5))


def prolong(field):
    first, second, third = field.shape
    spread = jnp.broadcast_to(field[:, None, :, None, :, None], (first, 2, second, 2, third, 2))
    return spread.reshape(first * 2, second * 2, third * 2)


def axis_layers(packed, axis_name, by):
    if axis_name == "gx":
        return passed_along(packed, "gx", by)
    if axis_name == "gy":
        return passed_along(packed, "gy", by)
    return passed_along(packed, "gz", by)


def extend_all(fields, margin):
    current = list(fields)
    for dim_index, axis_name in ((0, "gx"), (1, "gy"), (2, "gz")):
        lows = [lax.slice_in_dim(f, 0, margin, axis=dim_index) for f in current]
        highs = [
            lax.slice_in_dim(f, f.shape[dim_index] - margin, f.shape[dim_index], axis=dim_index)
            for f in current
        ]
        received = {}
        for by in (1, -1):
            pieces = highs if by == 1 else lows
            packed = jnp.concatenate([p.reshape(-1) for p in pieces])
            received[by] = axis_layers(packed, axis_name, by)
        grown = []
        offset = 0
        for index, field in enumerate(current):
            piece_shape = lows[index].shape
            count = lows[index].size
            from_lower = received[1][offset : offset + count].reshape(piece_shape)
            from_upper = received[-1][offset : offset + count].reshape(piece_shape)
            offset = offset + count
            grown.append(jnp.concatenate([from_lower, field, from_upper], axis=dim_index))
        current = grown
    return current


def smooth_merged(items):
    results = {}
    approxes = [damping * rhs / (6.0 * 0.25**lev) for rhs, lev in items]
    for sweep_index in range(SWEEPS - 1):
        padded_list = extend_all(approxes, 1)
        renewed = []
        for index, (rhs, lev) in enumerate(items):
            scaling = 0.25**lev
            diagonal_value = 6.0 * scaling
            renewed.append(
                approxes[index]
                + damping * (rhs - scaling * padded_stencil(padded_list[index])) / diagonal_value
            )
        approxes = renewed
    for index, (rhs, lev) in enumerate(items):
        results[lev] = approxes[index]
    return results


def precondition(residual):
    chain = [residual]
    for level_index in range(1, LEVELS):
        chain.append(restrict(chain[-1]))
    first_level = LEVELS - 1
    local_levels = list(range(first_level + 1))
    smoothed = smooth_merged([(chain[lev], lev) for lev in local_levels])
    correction = smoothed[first_level]
    for level_index in range(first_level - 1, -1, -1):
        correction = prolong(correction) + smoothed[level_index]
    return correction


def apply_fine(field):
    padded = padded_2(field, (("gx", 0), ("gy", 1), ("gz", 2)), 1)
    return padded_stencil(padded)


def shards(right_side, guess):
    solution_field = guess
    residual = right_side - apply_fine(guess)
    for step_index in range(STEPS):
        direction = precondition(residual)
        image = apply_fine(direction)
        along, curvature = lax.psum(
            (jnp.sum(residual * direction), jnp.sum(direction * image)), ("gx", "gy", "gz")
        )
        alpha = along / curvature
        solution_field = solution_field + alpha * direction
        residual = residual - alpha * image
    return (solution_field, residual)


def solution(mesh):
    placed = (P("gx", "gy", "gz"), P("gx", "gy", "gz"))
    return jax.shard_map(
        shards,
        mesh=mesh,
        in_specs=placed,
        out_specs=(P("gx", "gy", "gz"), P("gx", "gy", "gz")),
        check_vma=False,
    )
```

profile of v0, /device:TPU:0, one launch (start us, length us, event | category | flops | bytes accessed | tf_op | source)
XLA Modules:
  0.0 606.6 jit_solution(4249604036732145625)
XLA Ops:
  2.7 5.6 collective-permute-start.1
  17.2 4.5 collective-permute-start.5
  25.7 34.9 %reshape.1638 = f32[16,2,16,2,64,2]{5,4,3,2,1,0:T(8,128)} reshape(f32[32,32,128]{2,1,0:T(8,128)S(1)} %copy.405) | data formatting | bytes 1048576 | tf_op jit(solution)/shard_map/reshape | solution.py:42
  60.5 12.2 %reduce_sum.140 = f32[16,16,64]{2,1,0:T(8,128)S(1)} reduce(f32[16,2,16,2,64,2]{5,4,3,2,1,0:T(8,128)} %reshape.1638, f32[]{:T(128)} %constant.169.clone.1), dimensions={1,3,5}, to_apply=%region_0.0 | reduce | flops 114688 | bytes 589828 | tf_op jit(solution)/shard_map/reduce_sum | solution.py:43
  72.8 5.6 div.223
  97.4 5.7 collective-permute-done.8
  109.0 4.7 collective-permute-start.11
  128.3 4.4 collective-permute-done.12
  147.7 4.5 collective-permute-start.17
  170.4 4.4 collective-permute-done.18
  190.2 4.9 collective-permute-start.23
  204.2 4.9 reshape.1846
  210.7 11.4 %broadcast_in_dim.39 = f32[16,2,16,2,64,2]{5,4,3,2,1,0:T(8,128)} broadcast(f32[16,16,64]{2,1,0:T(8,128)S(1)} %fusion.112), dimensions={0,2,4} | broadcast | bytes 589824 | tf_op jit(solution)/shard_map/broadcast_in_dim | solution.py:48
  222.0 24.1 %reshape.1849 = f32[32,32,128]{2,1,0:T(8,128)S(1)} reshape(f32[16,2,16,2,64,2]{5,4,3,2,1,0:T(8,128)} %broadcast_in_dim.39) | data formatting | bytes 1048576 | tf_op jit(solution)/shard_map/reshape | solution.py:49
  250.0 4.5 collective-permute-start.25
  263.5 4.5 collective-permute-start.29
  271.1 45.0 %all-reduce.1 = (f32[]{:T(128)}, f32[]{:T(128)}) all-reduce(f32[]{:T(128)} %get-tuple-element.9, f32[]{:T(128)} %get-tuple-element.8), channel_id=1, replica_groups=mesh['gx'=4,'gy'=4,'gz'=2] {'gx','gy','gz'}, use_global_device_ids=true, to_apply=%region_7.0 | all-reduce | flops 2 | bytes 16 | tf_op jit(solution)/shard_map/psum | solution.py:129
  317.9 34.9 %reshape.1852 = f32[16,2,16,2,64,2]{5,4,3,2,1,0:T(8,128)} reshape(f32[32,32,128]{2,1,0:T(8,128)S(1)} %copy.511) | data formatting | bytes 1048576 | tf_op jit(solution)/shard_map/reshape | solution.py:42
  352.7 12.2 %reduce_sum.149 = f32[16,16,64]{2,1,0:T(8,128)S(1)} reduce(f32[16,2,16,2,64,2]{5,4,3,2,1,0:T(8,128)} %reshape.1852, f32[]{:T(128)} %constant.169.clone.1), dimensions={1,3,5}, to_apply=%region_10.0 | reduce | flops 114688 | bytes 589828 | tf_op jit(solution)/shard_map/reduce_sum | solution.py:43
  365.0 5.6 div.269
  378.1 4.3 collective-permute-done.30
  399.4 4.5 collective-permute-start.35
  416.4 4.3 collective-permute-done.36
  437.6 4.5 collective-permute-start.41
  455.9 4.4 collective-permute-done.42
  477.2 4.8 collective-permute-start.47
  488.1 4.9 reshape.2060
  493.8 11.4 %broadcast_in_dim.87 = f32[16,2,16,2,64,2]{5,4,3,2,1,0:T(8,128)} broadcast(f32[16,16,64]{2,1,0:T(8,128)S(1)} %fusion.81), dimensions={0,2,4} | broadcast | bytes 589824 | tf_op jit(solution)/shard_map/broadcast_in_dim | solution.py:48
  505.1 24.5 %reshape.2063 = f32[32,32,128]{2,1,0:T(8,128)} reshape(f32[16,2,16,2,64,2]{5,4,3,2,1,0:T(8,128)} %broadcast_in_dim.87) | data formatting | bytes 1048576 | tf_op jit(solution)/shard_map/reshape | solution.py:49
  533.8 4.5 collective-permute-start.49
  547.9 4.5 collective-permute-start.53
  556.4 44.8 %all-reduce = (f32[]{:T(128)}, f32[]{:T(128)}) all-reduce(f32[]{:T(128)} %get-tuple-element.7, f32[]{:T(128)} %get-tuple-element.6), channel_id=1, replica_groups=mesh['gx'=4,'gy'=4,'gz'=2] {'gx','gy','gz'}, use_global_device_ids=true, to_apply=%region_17.0 | all-reduce | flops 2 | bytes 16 | tf_op jit(solution)/shard_map/psum | solution.py:129
  (1040 shorter events, 240.0 us)
Async XLA Ops:
  1.4 8.2 %collective-permute-start = (f32[1,32,128]{2,0,1:T(1,128)S(1)}, f32[1,32,128]{2,0,1:T(1,128)S(1)}, u32[]{:S(2)}, u32[]{:S(2)}) collective-permute-start(f32[1,32,128]{2,0,1:T(1,128)S(1)} %bitcast.399), channel_id=1, source_target_pairs={{8,0},{16,8},{24,16},{9,1},{17,9},{25,17},{10,2},{18,10},{26,18},{... | collective-permute-start | bytes 49160 | tf_op jit(solution)/shard_map/ppermute | solution.py:28
  2.7 7.0 %collective-permute-start.1 = (f32[1,32,128]{2,0,1:T(1,128)S(1)}, f32[1,32,128]{2,0,1:T(1,128)S(1)}, u32[]{:S(2)}, u32[]{:S(2)}) collective-permute-start(f32[1,32,128]{2,0,1:T(1,128)S(1)} %bitcast.398), channel_id=1, source_target_pairs={{0,8},{8,16},{16,24},{1,9},{9,17},{17,25},{2,10},{10,18},{18,26},{... | collective-permute-start | bytes 49160 | tf_op jit(solution)/shard_map/ppermute | solution.py:27
  15.5 6.2 %collective-permute-start.4 = (f32[34,34,1]{1,2,0:T(1,128)S(1)}, f32[34,34,1]{1,2,0:T(1,128)S(1)}, u32[]{:S(2)}, u32[]{:S(2)}) collective-permute-start(f32[34,34,1]{1,2,0:T(1,128)S(1)} %copy.400), channel_id=1, source_target_pairs={{1,0},{3,2},{5,4},{7,6},{9,8},{11,10},{13,12},{15,14},{17,16},{19,... | collective-permute-start | bytes 13880 | tf_op jit(solution)/shard_map/ppermute | solution.py:28
  17.2 6.0 collective-permute-start.5
  82.3 5.9 collective-permute-start.7
  95.9 7.1 %collective-permute-start.8 = (f32[5964]{0:T(1024)S(1)}, f32[5964]{0:T(1024)S(1)}, u32[]{:S(2)}, u32[]{:S(2)}) collective-permute-start(f32[5964]{0:T(1024)S(1)} %concatenate.1027), channel_id=1, source_target_pairs={{2,0},{4,2},{6,4},{3,1},{5,3},{7,5},{10,8},{12,10},{14,12},{11,9},... | collective-permute-start | bytes 71576 | tf_op jit(solution)/shard_map/ppermute | solution.py:17
  106.6 7.2 %collective-permute-start.10 = (f32[1641]{0:T(1024)S(1)}, f32[1641]{0:T(1024)S(1)}, u32[]{:S(2)}, u32[]{:S(2)}) collective-permute-start(f32[1641]{0:T(1024)S(1)} %concatenate.1035), channel_id=1, source_target_pairs={{1,0},{3,2},{5,4},{7,6},{9,8},{11,10},{13,12},{15,14},{17,16},{19,... | collective-permute-start | bytes 19700 | tf_op jit(solution)/shard_map/ppermute | solution.py:17
  109.0 5.9 collective-permute-start.11
  122.3 5.9 collective-permute-start.13
  126.9 5.8 collective-permute-start.12
  145.3 7.0 %collective-permute-start.16 = (f32[1641]{0:T(1024)S(1)}, f32[1641]{0:T(1024)S(1)}, u32[]{:S(2)}, u32[]{:S(2)}) collective-permute-start(f32[1641]{0:T(1024)S(1)} %concatenate.1085), channel_id=1, source_target_pairs={{1,0},{3,2},{5,4},{7,6},{9,8},{11,10},{13,12},{15,14},{17,16},{19,... | collective-permute-start | bytes 19700 | tf_op jit(solution)/shard_map/ppermute | solution.py:17
  147.7 5.9 collective-permute-start.17
  163.2 7.2 %collective-permute-start.19 = (f32[5460]{0:T(1024)S(1)}, f32[5460]{0:T(1024)S(1)}, u32[]{:S(2)}, u32[]{:S(2)}) collective-permute-start(f32[5460]{0:T(1024)S(1)} %concatenate.1120), channel_id=1, source_target_pairs={{0,8},{8,16},{16,24},{1,9},{9,17},{17,25},{2,10},{10,18},{18,26},{... | collective-permute-start | bytes 65528 | tf_op jit(solution)/shard_map/ppermute | solution.py:17
  169.1 5.8 collective-permute-start.18
  187.7 7.4 %collective-permute-start.22 = (f32[1641]{0:T(1024)S(1)}, f32[1641]{0:T(1024)S(1)}, u32[]{:S(2)}, u32[]{:S(2)}) collective-permute-start(f32[1641]{0:T(1024)S(1)} %concatenate.1135), channel_id=1, source_target_pairs={{1,0},{3,2},{5,4},{7,6},{9,8},{11,10},{13,12},{15,14},{17,16},{19,... | collective-permute-start | bytes 19700 | tf_op jit(solution)/shard_map/ppermute | solution.py:17
  190.2 5.9 collective-permute-start.23
  248.7 5.9 collective-permute-start.24
  250.0 6.0 collective-permute-start.25
  261.8 6.2 %collective-permute-start.28 = (f32[34,34,1]{1,2,0:T(1,128)S(1)}, f32[34,34,1]{1,2,0:T(1,128)S(1)}, u32[]{:S(2)}, u32[]{:S(2)}) collective-permute-start(f32[34,34,1]{1,2,0:T(1,128)S(1)} %copy.506), channel_id=1, source_target_pairs={{1,0},{3,2},{5,4},{7,6},{9,8},{11,10},{13,12},{15,14},{17,16},{19,... | collective-permute-start | bytes 13880 | tf_op jit(solution)/shard_map/ppermute | solution.py:28
  263.5 6.0 collective-permute-start.29
  385.7 5.8 collective-permute-start.32
  397.0 7.0 %collective-permute-start.34 = (f32[1641]{0:T(1024)S(1)}, f32[1641]{0:T(1024)S(1)}, u32[]{:S(2)}, u32[]{:S(2)}) collective-permute-start(f32[1641]{0:T(1024)S(1)} %concatenate.1193), channel_id=1, source_target_pairs={{1,0},{3,2},{5,4},{7,6},{9,8},{11,10},{13,12},{15,14},{17,16},{19,... | collective-permute-start | bytes 19700 | tf_op jit(solution)/shard_map/ppermute | solution.py:17
  399.4 5.9 collective-permute-start.35
  435.2 7.0 %collective-permute-start.40 = (f32[1641]{0:T(1024)S(1)}, f32[1641]{0:T(1024)S(1)}, u32[]{:S(2)}, u32[]{:S(2)}) collective-permute-start(f32[1641]{0:T(1024)S(1)} %concatenate.1243), channel_id=1, source_target_pairs={{1,0},{3,2},{5,4},{7,6},{9,8},{11,10},{13,12},{15,14},{17,16},{19,... | collective-permute-start | bytes 19700 | tf_op jit(solution)/shard_map/ppermute | solution.py:17
  437.6 5.9 collective-permute-start.41
  454.5 5.8 collective-permute-start.42
  474.8 7.2 %collective-permute-start.46 = (f32[1641]{0:T(1024)S(1)}, f32[1641]{0:T(1024)S(1)}, u32[]{:S(2)}, u32[]{:S(2)}) collective-permute-start(f32[1641]{0:T(1024)S(1)} %concatenate.1293), channel_id=1, source_target_pairs={{1,0},{3,2},{5,4},{7,6},{9,8},{11,10},{13,12},{15,14},{17,16},{19,... | collective-permute-start | bytes 19700 | tf_op jit(solution)/shard_map/ppermute | solution.py:17
  477.2 5.9 collective-permute-start.47
  532.5 5.9 collective-permute-start.48
  533.8 6.0 collective-permute-start.49
  546.2 6.2 %collective-permute-start.52 = (f32[34,34,1]{1,2,0:T(1,128)S(1)}, f32[34,34,1]{1,2,0:T(1,128)S(1)}, u32[]{:S(2)}, u32[]{:S(2)}) collective-permute-start(f32[34,34,1]{1,2,0:T(1,128)S(1)} %copy.612), channel_id=1, source_target_pairs={{1,0},{3,2},{5,4},{7,6},{9,8},{11,10},{13,12},{15,14},{17,16},{19,... | collective-permute-start | bytes 13880 | tf_op jit(solution)/shard_map/ppermute | solution.py:28
  547.9 6.0 collective-permute-start.53
  (47 other events, 543.6 us)
where the time goes:
time: 617 us; the launch traced here: 607 us
  local copies, waits for them, and re-layouts  258 us (42%)
  starting transfers between devices  131 us (21%)
  blocking collectives  89.7 us (15%)
  waiting for transfers between devices  64.4 us (10%)
  other arithmetic  57.4 us (9%)
  between operations  6.56 us (1%)
    psum x2, blocking collectives, shards(): lax.psum((jnp.sum(residual * direction), jnp.sum(direction * image)), ('g...  89.7 us
    ppermute x36, starting transfers between devices, passed_along(): lax.ppermute(value, axis, [(source, source + steps) for source in range(f...  81.6 us
    reshape x2, local copies, waits for them, and re-layouts, restrict(): blocks = field.reshape(first // 2, 2, second // 2, 2, third // 2, 2)  69.7 us
    reshape x8, local copies, waits for them, and re-layouts, prolong(): return spread.reshape(first * 2, second * 2, third * 2)  58.9 us
    ppermute x36, waiting for transfers between devices, passed_along(): lax.ppermute(value, axis, [(source, source + steps) for source in range(f...  56 us
    ppermute x9, starting transfers between devices, padded_2(): before = lax.ppermute(last, axis, up)  37.4 us
    reduce_sum x12, other arithmetic, restrict(): return jnp.mean(blocks, axis=(1, 3, 5))  30.3 us
    broadcast_in_dim x12, local copies, waits for them, and re-layouts, prolong(): jnp.broadcast_to(field[:, None, :, None, :, None], (first, 2, second, 2,...  28.4 us
  transfers between devices with their start and end apart: 54, of which 27 were waited for; matrix products, arithmetic and copies ran while one was open for 3% of the time, Pallas kernels for 0%

commit v1 on v0

v1 whole, which is shorter than its diff:
```python
import jax
import jax.numpy as jnp
from jax import lax
from jax.experimental import pallas as pl
from jax.experimental.pallas import tpu as pltpu
from jax.sharding import PartitionSpec as P

LEVELS = 6
SWEEPS = 4
STEPS = 2
M = SWEEPS
HALO_LEVELS = 3
AXES = ("gx", "gy", "gz")
F32 = jnp.float32
HI = lax.Precision.HIGHEST


def up_to(value, unit):
    return -(-value // unit) * unit


def dot(a, b, dims=((1,), (0,))):
    return lax.dot_general(a, b, (dims, ((), ())), precision=HI, preferred_element_type=F32)


def iota(shape, dim):
    return lax.broadcasted_iota(jnp.int32, shape, dim)


def one(cond):
    return jnp.where(cond, 1.0, 0.0).astype(F32)


def signed(index, size, own):
    return jnp.where(index < own + M, index, index - size)


def cyclic(value, axis, by):
    count = lax.axis_size(axis)
    return lax.ppermute(value, axis, [(i, (i + by) % count) for i in range(count)])


class Plan:
    def __init__(self, local, counts):
        self.local, self.counts = local, counts
        self.own = [tuple(n >> l for n in local) for l in range(LEVELS)]
        self.whole = [tuple(n * c >> l for n, c in zip(local, counts)) for l in range(LEVELS)]
        self.lanes = up_to(local[2], 128)
        self.ring = []
        for l in range(LEVELS):
            if l < HALO_LEVELS:
                n = self.own[l]
                self.ring.append((n[0] + 2 * M, up_to(n[1] + 2 * M, 8), up_to(n[2] + 2 * M, 128)))
            else:
                n = self.whole[l]
                self.ring.append((n[0] + 1, up_to(n[1] + 1, 8), up_to(n[2] + 1, 128)))
        self.devices = counts[0] * counts[1] * counts[2]
        self.chunk = self.own[HALO_LEVELS][1]
        self.ext = [(n[0] + 2 * M, n[1] + 2 * M) for n in self.own[:HALO_LEVELS]]
        self.yrows = sum(n[0] * M for n in self.own[:HALO_LEVELS])
        self.xrows = sum(M * e[1] for e in self.ext)
        self.hcols = [up_to(e[0] * e[1], 128) for e in self.ext]


def restrict_to(plan, level, source, store):
    nx, ny, nz = plan.own[level]
    lanes = plan.lanes
    rz = one((iota((lanes, lanes), 0) >> 1 == iota((lanes, lanes), 1)) & (iota((lanes, lanes), 0) < nz))
    ry = one(iota((ny // 2, ny), 1) >> 1 == iota((ny // 2, ny), 0)) * 0.125
    pairs = jnp.sum(source[...].reshape(nx // 2, 2, ny, lanes), axis=1)
    across = dot(pairs.reshape(nx // 2 * ny, lanes), rz).reshape(nx // 2, ny, lanes)
    for i in range(nx // 2):
        store(i, dot(ry, across[i]))


def send_pack(plan, v, g1, g2, yl, yu, chunk, sums):
    lanes = plan.lanes

    def store1(i, u):
        g1[i] = u

    def store2(i, u):
        g2[i] = u

    restrict_to(plan, 0, v, store1)
    restrict_to(plan, 1, g1, store2)
    n3 = plan.own[3]
    parts = [jnp.zeros((n3[1], lanes), F32)]

    def store3(i, u):
        place = one(iota((lanes, lanes), 1) == iota((lanes, lanes), 0) + i * n3[2])
        place = jnp.where(iota((lanes, lanes), 0) < n3[2], place, 0.0)
        parts[0] = parts[0] + dot(u, place)

    restrict_to(plan, 2, g2, store3)
    payload = parts[0]
    if sums is not None:
        at = iota(payload.shape, 1)
        first = iota(payload.shape, 0) == 0
        payload = jnp.where((at == lanes - 2) & first, sums[0], payload)
        payload = jnp.where((at == lanes - 1) & first, sums[1], payload)
    for d in range(plan.devices):
        chunk[d * plan.chunk : (d + 1) * plan.chunk, :] = payload
    row = 0
    for l, f in enumerate((v, g1, g2)):
        nx, ny, _ = plan.own[l]
        for i in range(nx):
            yl[row : row + M, :] = f[i, 0:M, :]
            yu[row : row + M, :] = f[i, ny - M : ny, :]
            row += M


def inside(plan, idx, level, dim, ring_index):
    size = plan.ring[level][dim]
    if level < HALO_LEVELS:
        own = plan.own[level][dim]
        at = signed(ring_index, size, own) + idx[dim] * own
        ok = (at >= 0) & (at < plan.whole[level][dim])
        s = signed(ring_index, size, own)
        return ok & (s >= -M)
    return ring_index < plan.whole[level][dim]


def plane_mask(plan, idx, level):
    _, ry, rz = plan.ring[level]
    return one(
        inside(plan, idx, level, 1, iota((ry, rz), 0)) & inside(plan, idx, level, 2, iota((ry, rz), 1))
    )


def smooth(plan, idx, level, g, a, b):
    rx, ry, rz = plan.ring[level]
    m9 = plane_mask(plan, idx, level) * (1.0 / 9.0)
    source, target = g, a
    for sweep in range(SWEEPS - 1):

        def body(i, carry, source=source, target=target):
            f = source[i]
            before = source[jnp.where(i == 0, rx - 1, i - 1)]
            after = source[jnp.where(i == rx - 1, 0, i + 1)]
            beside = before + after + pltpu.roll(f, 1, 0) + pltpu.roll(f, ry - 1, 0)
            beside = beside + pltpu.roll(f, 1, 1) + pltpu.roll(f, rz - 1, 1)
            sx = one(inside(plan, idx, level, 0, i))
            target[i] = g[i] + (m9 * sx) * (3.0 * f + beside)
            return carry

        lax.fori_loop(0, rx, body, 0)
        source, target = target, (b if target is a else a)
    return source


def coarse_map(plan, idx, level, dim, fine, coarse):
    size = plan.ring[level][dim]
    if level < HALO_LEVELS:
        s = signed(fine, size, plan.own[level][dim])
        if level + 1 < HALO_LEVELS:
            up = s >> 1
            return jnp.where(up < 0, up + plan.ring[level + 1][dim], up) == coarse
        return (s + idx[dim] * plan.own[level][dim]) >> 1 == coarse
    return (fine >> 1 == coarse) & (fine < plan.whole[level][dim])


def add_prolonged(plan, idx, level, f, scale, zc, out):
    rx, ry, rz = plan.ring[level]
    cx, cy, cz = plan.ring[level + 1]
    pz = one(coarse_map(plan, idx, level, 2, iota((cz, rz), 1), iota((cz, rz), 0)))
    py = one(coarse_map(plan, idx, level, 1, iota((ry, cy), 0), iota((ry, cy), 1)))
    halo = level < HALO_LEVELS
    low = -1 if halo else 0
    high = plan.own[level][0] + 1 if halo else plan.whole[level][0]
    if level + 1 == HALO_LEVELS:
        for s in range(low, high):
            i = s % rx
            at = s + idx[0] * plan.own[level][0]
            ok = (at >= 0) & (at < plan.whole[level][0])
            c = jnp.clip(at >> 1, 0, plan.whole[level + 1][0] - 1)
            u = dot(py, dot(zc[c], pz))
            out[i] = scale * f[i] + one(ok) * u
        return
    spread = dot(zc[...].reshape(cx * cy, cz), pz).reshape(cx, cy, rz)
    for c in range(low >> 1, (high - 1 >> 1) + 1):
        u = dot(py, spread[c % cx])
        for s in (2 * c, 2 * c + 1):
            if low <= s < high:
                i = s % rx
                out[i] = scale * f[i] + u
    if not halo:
        for i in range(high, rx):
            out[i] = jnp.zeros((ry, rz), F32)


def faces_kernel(plan, guess, xl, xu, yl, yu, zf):
    nx, ny, nz = plan.local
    lanes = plan.lanes
    xl[...] = guess[0]
    xu[...] = guess[nx - 1]
    yl[...] = guess[:, 0, :]
    yu[...] = guess[:, ny - 1, :]
    at, row = iota((8, lanes), 1), iota((8, lanes), 0)
    pick = one(((row == 0) & (at == 0)) | ((row == 1) & (at == nz - 1)))
    zf[...] = dot(pick, guess[...].reshape(nx * ny, lanes), ((1,), (1,)))


def residual_kernel(plan, idx, b, guess, xlo, xhi, ylo, yhi, zlo, zhi, r, g1, g2, yl, yu, chunk, side):
    nx, ny, nz = plan.local
    lanes = plan.lanes
    cx, cy, cz = plan.counts
    has = lambda dim, upper: one(idx[dim] < plan.counts[dim] - 1 if upper else idx[dim] > 0)
    at, row = iota((8, lanes), 1), iota((8, lanes), 0)
    upper = one((row == 0) & (at == nz - 1)) * has(2, True)
    lower = one((row == 1) & (at == 0)) * has(2, False)
    side[...] = (dot(zhi[...], upper, ((0,), (0,))) + dot(zlo[...], lower, ((0,), (0,)))).reshape(nx, ny, lanes)
    ys, zs = iota((ny, lanes), 0), iota((ny, lanes), 1)
    not_low, not_high = one(zs > 0), one(zs < nz - 1)
    y_low, y_high = ys == 0, ys == ny - 1
    for i in range(nx):
        f = guess[i]
        before = guess[i - 1] if i else xlo[...] * has(0, False)
        after = guess[i + 1] if i < nx - 1 else xhi[...] * has(0, True)
        beside = before + after
        beside = beside + jnp.where(y_low, (ylo[i] * has(1, False))[None, :], pltpu.roll(f, 1, 0))
        beside = beside + jnp.where(y_high, (yhi[i] * has(1, True))[None, :], pltpu.roll(f, ny - 1, 0))
        beside = beside + pltpu.roll(f, 1, 1) * not_low + pltpu.roll(f, lanes - 1, 1) * not_high
        r[i] = b[i] - (6.0 * f - (beside + side[i]))
    send_pack(plan, r, g1, g2, yl, yu, chunk, None)


def ring_y_kernel(plan, v, g1, g2, ylo, yhi, a0, a1, a2, xl, xu):
    row, out = 0, 0
    for l, (f, a) in enumerate(((v, a0), (g1, a1), (g2, a2))):
        nx, ny, _ = plan.own[l]
        e = plan.ext[l][1]
        a[:, 0:ny, :] = f[...]
        for i in range(nx):
            a[i, ny : ny + M, :] = yhi[row : row + M, :]
            a[i, ny + M : ny + 2 * M, :] = ylo[row : row + M, :]
            row += M
        for i in range(M):
            xl[out : out + e, :] = a[i]
            xu[out : out + e, :] = a[nx - M + i]
            out += e


def ring_x_kernel(plan, a0, a1, a2, xlo, xhi, c0, c1, c2, h):
    row, col = 0, 0
    lanes = plan.lanes
    at, k = iota((8, lanes), 1), iota((8, lanes), 0)
    for l, (a, c) in enumerate(((a0, c0), (a1, c1), (a2, c2))):
        nx, ny, nz = plan.own[l]
        ex, e = plan.ext[l]
        c[0:nx] = a[...]
        for i in range(M):
            c[nx + i] = xhi[row : row + e, :]
            c[nx + M + i] = xlo[row : row + e, :]
            row += e
        pick = one(at == jnp.where(k < M, k, nz - 2 * M + k))
        h[:, col : col + ex * e] = dot(pick, c[...].reshape(ex * e, lanes), ((1,), (1,)))
        if plan.hcols[l] > ex * e:
            h[:, col + ex * e : col + plan.hcols[l]] = jnp.zeros((8, plan.hcols[l] - ex * e), F32)
        col += plan.hcols[l]


def total_sums(plan, chunks):
    rows = chunks.shape
    at = iota(rows, 1)
    first = iota(rows, 0) % plan.chunk == 0
    data = chunks[...]
    along = jnp.sum(jnp.where((at == plan.lanes - 2) & first, data, 0.0))
    curvature = jnp.sum(jnp.where((at == plan.lanes - 1) & first, data, 0.0))
    return along, curvature


def step_kernel(plan, last, *refs):
    nin = 7 if not last else 11
    idx, c0, c1, c2, hlo, hhi, chunks = refs[:7]
    old = refs[7:nin]
    outs = refs[nin:]
    if last:
        z_out, w_out, sums_out = outs[:3]
        scratch = outs[3:]
        rings = scratch[:4]
        scratch = scratch[4:]
    else:
        z_out, w_out, g1, g2, yl, yu, chunk = outs[:7]
        rings = outs[7:11]
        scratch = outs[11:]
    bufs = [scratch[2 * l : 2 * l + 2] for l in range(LEVELS)]
    g4, g5 = scratch[2 * LEVELS : 2 * LEVELS + 2]
    fields = list(rings) + [g4, g5]
    lanes = plan.lanes
    if last:
        along, curvature = total_sums(plan, chunks)
        alpha = along / curvature
    col = 0
    at, k = iota((8, lanes), 1), iota((8, lanes), 0)
    for l, c in enumerate((c0, c1, c2)):
        nx, ny, nz = plan.own[l]
        ex, e = plan.ext[l]
        rx, ry, rz = plan.ring[l]
        mask = plane_mask(plan, idx, l)
        base = rz - lanes
        want = jnp.where(k < M, nz + k - base, lanes - 2 * M + k)
        place = one(at == want)
        got = jnp.where(iota((8, ex * e), 0) < M, hhi[:, col : col + ex * e], hlo[:, col : col + ex * e])
        col += plan.hcols[l]
        tile = dot(got, place, ((0,), (0,))).reshape(ex, e, lanes)
        for i in range(rx):
            m = mask * one(inside(plan, idx, l, 0, jnp.int32(i)))
            if base:
                full = jnp.concatenate([c[i], tile[i]], axis=1)
            else:
                full = c[i] + tile[i]
            full = full * m
            rings[l][i] = old[l][i] - alpha * full if last else full
    n3 = plan.own[3]
    g3 = rings[3]
    g3[...] = jnp.zeros(g3.shape, F32)
    d = 0
    for ix in range(plan.counts[0]):
        for iy in range(plan.counts[1]):
            for iz in range(plan.counts[2]):
                part = chunks[d * plan.chunk : (d + 1) * plan.chunk, :]
                for i in range(n3[0]):
                    g3[
                        ix * n3[0] + i, iy * n3[1] : (iy + 1) * n3[1], iz * n3[2] : (iz + 1) * n3[2]
                    ] = part[:, i * n3[2] : (i + 1) * n3[2]]
                d += 1
    if last:
        g3[...] = old[3][...] - alpha * g3[...]
    for l in (3, 4):
        rx, ry, rz = plan.ring[l]
        cx, cy, cz = plan.ring[l + 1]
        rzm = one((iota((rz, cz), 0) >> 1 == iota((rz, cz), 1)) & (iota((rz, cz), 0) < plan.whole[l][2]))
        rym = one((iota((cy, ry), 1) >> 1 == iota((cy, ry), 0)) & (iota((cy, ry), 1) < plan.whole[l][1])) * 0.125
        for i in range(plan.whole[l + 1][0]):
            fields[l + 1][i] = dot(rym, dot(fields[l][2 * i] + fields[l][2 * i + 1], rzm))
        fields[l + 1][cx - 1] = jnp.zeros((cy, cz), F32)
    zc = None
    for l in range(LEVELS - 1, -1, -1):
        f = smooth(plan, idx, l, fields[l], *bufs[l])
        out = bufs[l][1] if f is bufs[l][0] else bufs[l][0]
        scale = 4.0**l / 9.0
        if zc is None:
            out[...] = scale * f[...]
        else:
            add_prolonged(plan, idx, l, f, scale, zc, out)
        zc = out
    nx, ny, nz = plan.local
    rx, ry, rz = plan.ring[0]
    first = jnp.zeros((ny, lanes), F32)
    second = jnp.zeros((ny, lanes), F32)

    def body(i, carry):
        first, second = carry
        f = zc[i]
        before = zc[jnp.where(i == 0, rx - 1, i - 1)]
        after = zc[i + 1]
        beside = before + after + pltpu.roll(f, 1, 0) + pltpu.roll(f, ry - 1, 0)
        beside = beside + pltpu.roll(f, 1, 1) + pltpu.roll(f, rz - 1, 1)
        w = (6.0 * f - beside)[:ny, :lanes]
        z = f[:ny, :lanes]
        z_out[i] = z
        w_out[i] = w
        return first + z * rings[0][i][:ny, :lanes], second + z * w

    first, second = lax.fori_loop(0, nx, body, (first, second))
    sums = (jnp.sum(first), jnp.sum(second))
    if last:
        row, at = iota(sums_out.shape, 0), iota(sums_out.shape, 1)
        sums_out[...] = jnp.where(at == lanes - 2, sums[0], jnp.where(at == lanes - 1, sums[1], 0.0))
    else:
        send_pack(plan, w_out, g1, g2, yl, yu, chunk, sums)


def final_kernel(plan, chunks1, chunks2, guess, r, z1, w1, z2, w2, x_out, r_out):
    along, curvature = total_sums(plan, chunks1)
    alpha1 = along / curvature
    data = chunks2[...]
    at = iota(data.shape, 1)
    along = jnp.sum(jnp.where(at == plan.lanes - 2, data, 0.0))
    curvature = jnp.sum(jnp.where(at == plan.lanes - 1, data, 0.0))
    alpha2 = along / curvature
    x_out[...] = guess[...] + alpha1 * z1[...] + alpha2 * z2[...]
    r_out[...] = r[...] - alpha1 * w1[...] - alpha2 * w2[...]


def sds(*shape):
    return jax.ShapeDtypeStruct(shape, F32)


def call(body, outs, args, scratch=(), smem=False):
    specs = [pl.BlockSpec(memory_space=pltpu.VMEM)] * len(args)
    if smem:
        specs[0] = pl.BlockSpec(memory_space=pltpu.SMEM)
    return pl.pallas_call(
        body,
        out_shape=tuple(outs),
        in_specs=specs,
        out_specs=tuple(pl.BlockSpec(memory_space=pltpu.VMEM) for _ in outs),
        scratch_shapes=list(scratch),
    )(*args)


def exchange(value_low, value_high, axis):
    return cyclic(value_high, axis, 1), cyclic(value_low, axis, -1)


def shards(right_side, guess):
    counts = tuple(lax.axis_size(a) for a in AXES)
    plan = Plan(right_side.shape, counts)
    nx, ny, nz = plan.local
    lanes = plan.lanes
    idx = jnp.stack([lax.axis_index(a) for a in AXES]).astype(jnp.int32)
    bind = lambda f, *extra: lambda *refs: f(plan, *extra, *refs)
    own = [sds(*n[:2], lanes) for n in plan.own[:HALO_LEVELS]]
    packs = [own[1], own[2], sds(plan.yrows, lanes), sds(plan.yrows, lanes), sds(plan.devices * plan.chunk, lanes)]

    xl, xu, yl, yu, zf = call(
        bind(faces_kernel), [sds(ny, lanes), sds(ny, lanes), sds(nx, lanes), sds(nx, lanes), sds(8, nx * ny)], [guess]
    )
    xlo, xhi = exchange(xl, xu, "gx")
    ylo, yhi = exchange(yl, yu, "gy")
    zlo, zhi = swap(zf)
    r, g1, g2, yl, yu, chunk = call(
        bind(residual_kernel),
        [own[0]] + packs,
        [idx, right_side, guess, xlo, xhi, ylo, yhi, zlo, zhi],
        [pltpu.VMEM((nx, ny, lanes), F32)],
        smem=True,
    )
    rings = [sds(*s) for s in plan.ring[:4]]
    as_scratch = lambda items: [pltpu.VMEM(s.shape, F32) for s in items]
    work = [pltpu.VMEM(s, F32) for s in plan.ring for _ in range(2)]
    work += [pltpu.VMEM(s, F32) for s in plan.ring[4:6]]
    field, old = r, []
    kept = []
    for step in range(STEPS):
        last = step == STEPS - 1
        chunks = lax.all_to_all(chunk, AXES, 0, 0, tiled=True)
        ylo, yhi = exchange(yl, yu, "gy")
        *a, xl, xu = call(
            bind(ring_y_kernel),
            [sds(n[0], e[1], lanes) for n, e in zip(plan.own, plan.ext)] + [sds(plan.xrows, lanes)] * 2,
            [field, g1, g2, ylo, yhi],
        )
        xlo, xhi = exchange(xl, xu, "gx")
        *c, h = call(
            bind(ring_x_kernel),
            [sds(*e, lanes) for e in plan.ext] + [sds(8, sum(plan.hcols))],
            [*a, xlo, xhi],
        )
        hlo, hhi = swap(h)
        args = [idx, *c, hlo, hhi, chunks, *old]
        if last:
            z, w, sums = call(
                bind(step_kernel, True), [own[0], own[0], sds(plan.devices, lanes)], args, as_scratch(rings) + work, smem=True
            )
        else:
            z, w, g1, g2, yl, yu, chunk, *old = call(
                bind(step_kernel, False), [own[0], own[0]] + packs + rings, args, work, smem=True
            )
            field = w
        kept.append((z, w, chunks))
    sums = lax.all_to_all(sums, AXES, 0, 0, tiled=True)
    (z1, w1, _), (z2, w2, chunks1) = kept
    return call(bind(final_kernel), [own[0], own[0]], [chunks1, sums, guess, r, z1, w1, z2, w2])


def swap(h):
    low = cyclic(h, "gz", 1)
    return (low, low) if lax.axis_size("gz") == 2 else (low, cyclic(h, "gz", -1))


def solution(mesh):
    placed = P("gx", "gy", "gz")
    return jax.shard_map(shards, mesh=mesh, in_specs=(placed, placed), out_specs=(placed, placed), check_vma=False)
```

time: 617 us -> 181 us (0.29); the launches traced: 607 us -> 181 us
  local copies, waits for them, and re-layouts: 258 us -> 4.46 us
  Pallas kernels: 0 us -> 111 us
  starting transfers between devices: 131 us -> 28.5 us
  blocking collectives: 89.7 us -> 11.5 us
  other arithmetic: 57.4 us -> 0.6 us
  waiting for transfers between devices: 64.4 us -> 23.6 us
    reshape x400 -> x0, local copies, waits for them, and re-layouts: 173 us -> none  [the longest x2 69.7 us: restrict(): blocks = field.reshape(first // 2, 2, second // 2, 2, third // 2, 2)]
    pallas_call x0 -> x9, Pallas kernels: none -> 111 us  [call(): pl.pallas_call(body, out_shape=tuple(outs), in_specs=specs, out_specs=tup...]
    ppermute x54 -> x15, starting transfers between devices: 131 us -> 22.7 us  [cyclic(): lax.ppermute(value, axis, [(i, (i + by) % count) for i in range(count)])]
    psum x2 -> x0, blocking collectives: 89.7 us -> none  [shards(): lax.psum((jnp.sum(residual * direction), jnp.sum(direction * image)), ('g...]
    ppermute x54 -> x15, waiting for transfers between devices: 64.4 us -> 23.6 us  [cyclic(): lax.ppermute(value, axis, [(i, (i + by) % count) for i in range(count)])]
    reduce_sum x14 -> x0, other arithmetic: 33.6 us -> none  [the longest x12 30.3 us: restrict(): return jnp.mean(blocks, axis=(1, 3, 5))]
    slice x288 -> x0, local copies, waits for them, and re-layouts: 31.9 us -> none  [the longest x48 14.8 us: extend_all(): lows = [lax.slice_in_dim(f, 0, margin, axis=dim_index) for f in current]]
    broadcast_in_dim x12 -> x0, local copies, waits for them, and re-layouts: 28.4 us -> none  [prolong(): jnp.broadcast_to(field[:, None, :, None, :, None], (first, 2, second, 2,...]
  transfers between devices with their start and end apart: 54 -> 17, of which waited for: 27 -> 11; matrix products, arithmetic and copies ran while one was open for 3% -> 0% of each run, Pallas kernels for 0% -> 3%
where the time goes in v1:
time: 181 us
  Pallas kernels  111 us (61%)
  starting transfers between devices  28.5 us (16%)
  waiting for transfers between devices  23.6 us (13%)
  blocking collectives  11.5 us (6%)
  local copies, waits for them, and re-layouts  4.46 us (2%)
    pallas_call x9, Pallas kernels, call(): pl.pallas_call(body, out_shape=tuple(outs), in_specs=specs, out_specs=tup...  111 us
    ppermute x15, waiting for transfers between devices, cyclic(): lax.ppermute(value, axis, [(i, (i + by) % count) for i in range(count)])  23.6 us
    ppermute x15, starting transfers between devices, cyclic(): lax.ppermute(value, axis, [(i, (i + by) % count) for i in range(count)])  22.7 us
    all_to_all x1, blocking collectives, shards(): sums = lax.all_to_all(sums, AXES, 0, 0, tiled=True)  11.5 us
    all_to_all x2, starting transfers between devices, shards(): chunks = lax.all_to_all(chunk, AXES, 0, 0, tiled=True)  5.78 us
    unnamed x34, local copies, waits for them, and re-layouts  4.46 us
  transfers between devices with their start and end apart: 17, of which 11 were waited for; matrix products, arithmetic and copies ran while one was open for 0% of the time, Pallas kernels for 3%

profile of v1, /device:TPU:0, one launch (start us, length us, event | category | flops | bytes accessed | tf_op | source)
XLA Modules:
  0.0 180.9 jit_solution(5221460712463795538)
XLA Ops:
  0.6 2.2 %shard_map.41 = (f32[32,128]{1,0:T(8,128)}, f32[32,128]{1,0:T(8,128)}, f32[32,128]{1,0:T(8,128)}, f32[32,128]{1,0:T(8,128)}, f32[8,1024]{1,0:T(8,128)}) custom-call(f32[32,32,128]{2,1,0:T(8,128)} %refs_2_.3), custom_call_target="tpu_custom_call" | custom-call | tf_op jit(solution)/shard_map/pallas_call | solution.py:395
  2.8 3.1 %collective-permute-start = (f32[32,128]{1,0:T(8,128)}, f32[32,128]{1,0:T(8,128)S(1)}, u32[]{:S(2)}, u32[]{:S(2)}) collective-permute-start(f32[32,128]{1,0:T(8,128)} %get-tuple-element.45), channel_id=1, source_target_pairs={{0,8},{8,16},{16,24},{24,0},{1,9},{9,17},{17,25},{25,1},{2,10},{10... | collective-permute-start | bytes 49160 | tf_op jit(solution)/shard_map/ppermute | solution.py:40
  5.9 2.0 %collective-permute-start.1 = (f32[32,128]{1,0:T(8,128)}, f32[32,128]{1,0:T(8,128)S(1)}, u32[]{:S(2)}, u32[]{:S(2)}) collective-permute-start(f32[32,128]{1,0:T(8,128)} %get-tuple-element.46), channel_id=1, source_target_pairs={{0,24},{8,0},{16,8},{24,16},{1,25},{9,1},{17,9},{25,17},{2,26},{10... | collective-permute-start | bytes 49160 | tf_op jit(solution)/shard_map/ppermute | solution.py:40
  7.9 1.7 collective-permute-start.3
  9.6 1.7 collective-permute-start.4
  12.0 1.8 collective-permute-done.4.refs_7_.refs_8_
  14.4 6.0 %shard_map.42 = (f32[32,32,128]{2,1,0:T(8,128)}, f32[16,16,128]{2,1,0:T(8,128)}, f32[8,8,128]{2,1,0:T(8,128)}, f32[224,128]{1,0:T(8,128)}, f32[224,128]{1,0:T(8,128)}, /*index=5*/f32[128,128]{1,0:T(8,128)}) custom-call(s32[3]{0:T(128)} %pad_add_fusion.refs_0_, f32[32,32,128]{2,1,0:T(8,128)} %refs_1_.1, f32[32,32,128]{2,1,0:T(8,128)} %refs_2_.3, ...), custom_call_target="tpu_custom_call" | custom-call | tf_op jit(solution)/shard_map/pallas_call | solution.py:395
  20.4 1.7 collective-permute-start.6
  22.1 2.7 %collective-permute-done.5.refs_3_ = f32[224,128]{1,0:T(8,128)S(1)} collective-permute-done((f32[224,128]{1,0:T(8,128)}, f32[224,128]{1,0:T(8,128)S(1)}, u32[]{:S(2)}, u32[]{:S(2)}) %collective-permute-start.5) | collective-permute-done | bytes 114720 | tf_op jit(solution)/shard_map/ppermute | solution.py:40
  26.1 2.2 %shard_map.43 = (f32[32,40,128]{2,1,0:T(8,128)}, f32[16,24,128]{2,1,0:T(8,128)}, f32[8,16,128]{2,1,0:T(8,128)}, f32[320,128]{1,0:T(8,128)}, f32[320,128]{1,0:T(8,128)}) custom-call(f32[32,32,128]{2,1,0:T(8,128)} %get-tuple-element.50.refs_0_.refs_3_, f32[16,16,128]{2,1,0:T(8,128)} %get-tuple-element.51.refs_1_, f32[8,8,128]{2,1,0:T(8,128)} %get-tuple-element.52.refs_2_, ...), custom_call_target="tpu_custom_call" | custom-call | tf_op jit(solution)/shard_map/pallas_call | solution.py:395
  28.3 3.8 %collective-permute-start.8 = (f32[320,128]{1,0:T(8,128)}, f32[320,128]{1,0:T(8,128)S(1)}, u32[]{:S(2)}, u32[]{:S(2)}) collective-permute-start(f32[320,128]{1,0:T(8,128)} %get-tuple-element.59), channel_id=1, source_target_pairs={{0,24},{8,0},{16,8},{24,16},{1,25},{9,1},{17,9},{25,17},{2,26},{10... | collective-permute-start | bytes 491528 | tf_op jit(solution)/shard_map/ppermute | solution.py:40
  32.1 2.9 %all-to-all-start = ((f32[32,4,128]{2,1,0:T(4,128)}), f32[32,4,128]{2,1,0:T(4,128)S(1)}, u32[]{:S(2)}, u32[]{:S(2)}) async-start(f32[32,4,128]{2,1,0:T(4,128)} %bitcast.16), calls=%async_computation | async-start | bytes 131072 | tf_op jit(solution)/shard_map/all_to_all | solution.py:439
  35.0 2.1 %collective-permute-done.7.refs_3_ = f32[320,128]{1,0:T(8,128)S(1)} collective-permute-done((f32[320,128]{1,0:T(8,128)}, f32[320,128]{1,0:T(8,128)S(1)}, u32[]{:S(2)}, u32[]{:S(2)}) %collective-permute-start.7) | collective-permute-done | bytes 163872 | tf_op jit(solution)/shard_map/ppermute | solution.py:40
  37.2 1.6 collective-permute-done.8.refs_4_
  39.5 3.1 %shard_map.44 = (f32[40,40,128]{2,1,0:T(8,128)}, f32[24,24,128]{2,1,0:T(8,128)}, f32[16,16,128]{2,1,0:T(8,128)}, f32[8,2560]{1,0:T(8,128)}) custom-call(f32[32,40,128]{2,1,0:T(8,128)} %get-tuple-element.55.refs_0_, f32[16,24,128]{2,1,0:T(8,128)} %get-tuple-element.56.refs_1_, f32[8,16,128]{2,1,0:T(8,128)} %get-tuple-element.57.refs_2_, ...), custom_call_target="tpu_custom_call" | custom-call | tf_op jit(solution)/shard_map/pallas_call | solution.py:395
  42.5 1.5 collective-permute-start.9
  44.0 3.6 %collective-permute-done.9.refs_4_.refs_5_ = f32[8,2560]{1,0:T(8,128)S(1)} collective-permute-done((f32[8,2560]{1,0:T(8,128)}, f32[8,2560]{1,0:T(8,128)S(1)}, u32[]{:S(2)}, u32[]{:S(2)}) %collective-permute-start.9) | collective-permute-done | bytes 81952 | tf_op jit(solution)/shard_map/ppermute | solution.py:40
  48.3 45.4 %shard_map.45 = (f32[32,32,128]{2,1,0:T(8,128)}, f32[32,32,128]{2,1,0:T(8,128)}, f32[16,16,128]{2,1,0:T(8,128)}, f32[8,8,128]{2,1,0:T(8,128)}, f32[224,128]{1,0:...) custom-call(s32[3]{0:T(128)} %pad_add_fusion.refs_0_, ...), custom_call_target="tpu_custom_call" | custom-call | tf_op jit(solution)/shard_map/pallas_call | solution.py:395
  93.8 1.7 collective-permute-start.11
  95.5 2.7 %collective-permute-done.10.refs_3_ = f32[224,128]{1,0:T(8,128)S(1)} collective-permute-done((f32[224,128]{1,0:T(8,128)}, f32[224,128]{1,0:T(8,128)S(1)}, u32[]{:S(2)}, u32[]{:S(2)}) %collective-permute-start.10) | collective-permute-done | bytes 114720 | tf_op jit(solution)/shard_map/ppermute | solution.py:40
  99.0 2.2 %shard_map.46 = (f32[32,40,128]{2,1,0:T(8,128)}, f32[16,24,128]{2,1,0:T(8,128)}, f32[8,16,128]{2,1,0:T(8,128)}, f32[320,128]{1,0:T(8,128)}, f32[320,128]{1,0:T(8,128)}) custom-call(f32[32,32,128]{2,1,0:T(8,128)} %get-tuple-element.66.refs_0_.refs_5_, f32[16,16,128]{2,1,0:T(8,128)} %get-tuple-element.67.refs_1_, f32[8,8,128]{2,1,0:T(8,128)} %get-tuple-element.68.refs_2_, ...), custom_call_target="tpu_custom_call" | custom-call | tf_op jit(solution)/shard_map/pallas_call | solution.py:395
  101.2 1.2 collective-permute-start.12
  102.4 2.7 %collective-permute-start.13 = (f32[320,128]{1,0:T(8,128)}, f32[320,128]{1,0:T(8,128)S(1)}, u32[]{:S(2)}, u32[]{:S(2)}) collective-permute-start(f32[320,128]{1,0:T(8,128)} %get-tuple-element.75), channel_id=1, source_target_pairs={{0,24},{8,0},{16,8},{24,16},{1,25},{9,1},{17,9},{25,17},{2,26},{10... | collective-permute-start | bytes 491528 | tf_op jit(solution)/shard_map/ppermute | solution.py:40
  105.0 2.9 %all-to-all-start.1 = ((f32[32,4,128]{2,1,0:T(4,128)}), f32[32,4,128]{2,1,0:T(4,128)S(1)}, u32[]{:S(2)}, u32[]{:S(2)}) async-start(f32[32,4,128]{2,1,0:T(4,128)} %bitcast.15), calls=%async_computation.1 | async-start | bytes 131072 | tf_op jit(solution)/shard_map/all_to_all | solution.py:439
  107.9 2.2 %collective-permute-done.12.refs_3_ = f32[320,128]{1,0:T(8,128)S(1)} collective-permute-done((f32[320,128]{1,0:T(8,128)}, f32[320,128]{1,0:T(8,128)S(1)}, u32[]{:S(2)}, u32[]{:S(2)}) %collective-permute-start.12) | collective-permute-done | bytes 163872 | tf_op jit(solution)/shard_map/ppermute | solution.py:40
  110.1 2.8 %collective-permute-done.13.refs_4_ = f32[320,128]{1,0:T(8,128)S(1)} collective-permute-done((f32[320,128]{1,0:T(8,128)}, f32[320,128]{1,0:T(8,128)S(1)}, u32[]{:S(2)}, u32[]{:S(2)}) %collective-permute-start.13) | collective-permute-done | bytes 163872 | tf_op jit(solution)/shard_map/ppermute | solution.py:40
  113.6 3.1 %shard_map.47 = (f32[40,40,128]{2,1,0:T(8,128)}, f32[24,24,128]{2,1,0:T(8,128)}, f32[16,16,128]{2,1,0:T(8,128)}, f32[8,2560]{1,0:T(8,128)}) custom-call(f32[32,40,128]{2,1,0:T(8,128)} %get-tuple-element.71.refs_0_, f32[16,24,128]{2,1,0:T(8,128)} %get-tuple-element.72.refs_1_, f32[8,16,128]{2,1,0:T(8,128)} %get-tuple-element.73.refs_2_, ...), custom_call_target="tpu_custom_call" | custom-call | tf_op jit(solution)/shard_map/pallas_call | solution.py:395
  116.7 1.5 collective-permute-start.14
  118.2 3.3 %collective-permute-done.14.refs_4_.refs_5_ = f32[8,2560]{1,0:T(8,128)S(1)} collective-permute-done((f32[8,2560]{1,0:T(8,128)}, f32[8,2560]{1,0:T(8,128)S(1)}, u32[]{:S(2)}, u32[]{:S(2)}) %collective-permute-start.14) | collective-permute-done | bytes 81952 | tf_op jit(solution)/shard_map/ppermute | solution.py:40
  122.2 44.0 %shard_map.48 = (f32[32,32,128]{2,1,0:T(8,128)}, f32[32,32,128]{2,1,0:T(8,128)}, f32[32,128]{1,0:T(8,128)}) custom-call(s32[3]{0:T(128)} %pad_add_fusion.refs_0_, f32[40,40,128]{2,1,0:T(8,128)} %get-tuple-element.76.refs_1_, f32[24,24,128]{2,1,0:T(8,128)} %get-tuple-element.77.refs_2_, f32[16,16,128]{2,1,0:T(8,128)} %get-tuple-element.78.refs_3_, ...), custom_call_target="tpu_custom_call" | custom-call | tf_op jit(solution)/shard_map/pallas_call | solution.py:395
  166.2 11.5 %all_to_all.33 = f32[32,1,128]{2,1,0:T(1,128)} all-to-all(f32[32,1,128]{2,1,0:T(1,128)} %bitcast.17), channel_id=1, replica_groups=mesh['gx'=4,'gy'=4,'gz'=2] {'gx','gy','gz'}, dimensions={0} | all-to-all | bytes 32768 | tf_op jit(solution)/shard_map/all_to_all | solution.py:464
  177.7 3.2 %shard_map.49 = (f32[32,32,128]{2,1,0:T(8,128)}, f32[32,32,128]{2,1,0:T(8,128)}) custom-call(f32[128,128]{1,0:T(8,128)} %bitcast.12, f32[32,128]{1,0:T(8,128)} %bitcast.14, f32[32,32,128]{2,1,0:T(8,128)} %refs_2_.3, f32[32,32,128]{2,1,0:T(8,128)} %get-tuple-element.50.refs_0_.refs_3_, f32[32,32,128]{2,1,0:T(8,128)} %get-tuple-element.85.refs_4_, ...), custom_call_target="tpu_custom_call" | custom-call | tf_op jit(solution)/shard_map/pallas_call | solution.py:395
  (47 shorter events, 5.8 us)
Async XLA Ops:
  2.8 9.1 %collective-permute-start = (f32[32,128]{1,0:T(8,128)}, f32[32,128]{1,0:T(8,128)S(1)}, u32[]{:S(2)}, u32[]{:S(2)}) collective-permute-start(f32[32,128]{1,0:T(8,128)} %get-tuple-element.45), channel_id=1, source_target_pairs={{0,8},{8,16},{16,24},{24,0},{1,9},{9,17},{17,25},{25,1},{2,10},{10... | collective-permute-start | bytes 49160 | tf_op jit(solution)/shard_map/ppermute | solution.py:40
  5.9 6.1 %collective-permute-start.1 = (f32[32,128]{1,0:T(8,128)}, f32[32,128]{1,0:T(8,128)S(1)}, u32[]{:S(2)}, u32[]{:S(2)}) collective-permute-start(f32[32,128]{1,0:T(8,128)} %get-tuple-element.46), channel_id=1, source_target_pairs={{0,24},{8,0},{16,8},{24,16},{1,25},{9,1},{17,9},{25,17},{2,26},{10... | collective-permute-start | bytes 49160 | tf_op jit(solution)/shard_map/ppermute | solution.py:40
  7.9 4.1 %collective-permute-start.2 = (f32[32,128]{1,0:T(8,128)}, f32[32,128]{1,0:T(8,128)S(1)}, u32[]{:S(2)}, u32[]{:S(2)}) collective-permute-start(f32[32,128]{1,0:T(8,128)} %get-tuple-element.47), channel_id=1, source_target_pairs={{0,2},{2,4},{4,6},{6,0},{1,3},{3,5},{5,7},{7,1},{8,10},{10,12},{12... | collective-permute-start | bytes 49160 | tf_op jit(solution)/shard_map/ppermute | solution.py:40
  7.9 4.1 %collective-permute-start.3 = (f32[32,128]{1,0:T(8,128)}, f32[32,128]{1,0:T(8,128)S(1)}, u32[]{:S(2)}, u32[]{:S(2)}) collective-permute-start(f32[32,128]{1,0:T(8,128)} %get-tuple-element.48), channel_id=1, source_target_pairs={{0,6},{2,0},{4,2},{6,4},{1,7},{3,1},{5,3},{7,5},{8,14},{10,8},{12,... | collective-permute-start | bytes 49160 | tf_op jit(solution)/shard_map/ppermute | solution.py:40
  9.6 4.1 %collective-permute-start.4 = (f32[8,1024]{1,0:T(8,128)}, f32[8,1024]{1,0:T(8,128)S(1)}, u32[]{:S(2)}, u32[]{:S(2)}) collective-permute-start(f32[8,1024]{1,0:T(8,128)} %get-tuple-element.49), channel_id=1, source_target_pairs={{0,1},{1,0},{2,3},{3,2},{4,5},{5,4},{6,7},{7,6},{8,9},{9,8},{10,11... | collective-permute-start | bytes 98312 | tf_op jit(solution)/shard_map/ppermute | solution.py:40
  12.0 1.8 %copy-start.13 = (f32[32,128]{1,0:T(8,128)}, f32[32,128]{1,0:T(8,128)S(1)}, u32[]{:S(2)}) copy-start(f32[32,128]{1,0:T(8,128)S(1)} %collective-permute-done.refs_3_) | copy-start | bytes 49156
  12.0 1.8 copy-start.14
  12.0 1.8 copy-start.15
  12.0 1.8 copy-start.16
  20.4 4.4 %collective-permute-start.5 = (f32[224,128]{1,0:T(8,128)}, f32[224,128]{1,0:T(8,128)S(1)}, u32[]{:S(2)}, u32[]{:S(2)}) collective-permute-start(f32[224,128]{1,0:T(8,128)} %get-tuple-element.53), channel_id=1, source_target_pairs={{0,2},{2,4},{4,6},{6,0},{1,3},{3,5},{5,7},{7,1},{8,10},{10,12},{12... | collective-permute-start | bytes 344072 | tf_op jit(solution)/shard_map/ppermute | solution.py:40
  20.4 5.0 %collective-permute-start.6 = (f32[224,128]{1,0:T(8,128)}, f32[224,128]{1,0:T(8,128)S(1)}, u32[]{:S(2)}, u32[]{:S(2)}) collective-permute-start(f32[224,128]{1,0:T(8,128)} %get-tuple-element.54), channel_id=1, source_target_pairs={{0,6},{2,0},{4,2},{6,4},{1,7},{3,1},{5,3},{7,5},{8,14},{10,8},{12,... | collective-permute-start | bytes 344072 | tf_op jit(solution)/shard_map/ppermute | solution.py:40
  24.8 0.6 copy-start.9
  25.4 0.6 copy-start.11
  28.3 8.9 %collective-permute-start.7 = (f32[320,128]{1,0:T(8,128)}, f32[320,128]{1,0:T(8,128)S(1)}, u32[]{:S(2)}, u32[]{:S(2)}) collective-permute-start(f32[320,128]{1,0:T(8,128)} %get-tuple-element.58), channel_id=1, source_target_pairs={{0,8},{8,16},{16,24},{24,0},{1,9},{9,17},{17,25},{25,1},{2,10},{10... | collective-permute-start | bytes 491528 | tf_op jit(solution)/shard_map/ppermute | solution.py:40
  28.3 10.5 %collective-permute-start.8 = (f32[320,128]{1,0:T(8,128)}, f32[320,128]{1,0:T(8,128)S(1)}, u32[]{:S(2)}, u32[]{:S(2)}) collective-permute-start(f32[320,128]{1,0:T(8,128)} %get-tuple-element.59), channel_id=1, source_target_pairs={{0,24},{8,0},{16,8},{24,16},{1,25},{9,1},{17,9},{25,17},{2,26},{10... | collective-permute-start | bytes 491528 | tf_op jit(solution)/shard_map/ppermute | solution.py:40
  32.1 11.9 %all-to-all-start = ((f32[32,4,128]{2,1,0:T(4,128)}), f32[32,4,128]{2,1,0:T(4,128)S(1)}, u32[]{:S(2)}, u32[]{:S(2)}) async-start(f32[32,4,128]{2,1,0:T(4,128)} %bitcast.16), calls=%async_computation | async-start | bytes 131072 | tf_op jit(solution)/shard_map/all_to_all | solution.py:439
  37.2 1.6 copy-start.4
  38.8 0.7 copy-start.6
  42.5 5.1 %collective-permute-start.9 = (f32[8,2560]{1,0:T(8,128)}, f32[8,2560]{1,0:T(8,128)S(1)}, u32[]{:S(2)}, u32[]{:S(2)}) collective-permute-start(f32[8,2560]{1,0:T(8,128)} %get-tuple-element.63), channel_id=1, source_target_pairs={{0,1},{1,0},{2,3},{3,2},{4,5},{5,4},{6,7},{7,6},{8,9},{9,8},{10,11... | collective-permute-start | bytes 245768 | tf_op jit(solution)/shard_map/ppermute | solution.py:40
  44.0 3.7 %copy-start.3 = (f32[32,4,128]{2,1,0:T(4,128)}, f32[32,4,128]{2,1,0:T(4,128)S(1)}, u32[]{:S(2)}) copy-start(f32[32,4,128]{2,1,0:T(4,128)S(1)} %all-to-all-done) | copy-start | bytes 196612
  47.7 0.6 copy-start.1
  93.8 4.4 %collective-permute-start.10 = (f32[224,128]{1,0:T(8,128)}, f32[224,128]{1,0:T(8,128)S(1)}, u32[]{:S(2)}, u32[]{:S(2)}) collective-permute-start(f32[224,128]{1,0:T(8,128)} %get-tuple-element.69), channel_id=1, source_target_pairs={{0,2},{2,4},{4,6},{6,0},{1,3},{3,5},{5,7},{7,1},{8,10},{10,12},{12... | collective-permute-start | bytes 344072 | tf_op jit(solution)/shard_map/ppermute | solution.py:40
  93.8 4.6 %collective-permute-start.11 = (f32[224,128]{1,0:T(8,128)}, f32[224,128]{1,0:T(8,128)S(1)}, u32[]{:S(2)}, u32[]{:S(2)}) collective-permute-start(f32[224,128]{1,0:T(8,128)} %get-tuple-element.70), channel_id=1, source_target_pairs={{0,6},{2,0},{4,2},{6,4},{1,7},{3,1},{5,3},{7,5},{8,14},{10,8},{12,... | collective-permute-start | bytes 344072 | tf_op jit(solution)/shard_map/ppermute | solution.py:40
  98.2 0.6 copy-start.10
  98.3 0.6 copy-start.12
  101.2 8.9 %collective-permute-start.12 = (f32[320,128]{1,0:T(8,128)}, f32[320,128]{1,0:T(8,128)S(1)}, u32[]{:S(2)}, u32[]{:S(2)}) collective-permute-start(f32[320,128]{1,0:T(8,128)} %get-tuple-element.74), channel_id=1, source_target_pairs={{0,8},{8,16},{16,24},{24,0},{1,9},{9,17},{17,25},{25,1},{2,10},{10... | collective-permute-start | bytes 491528 | tf_op jit(solution)/shard_map/ppermute | solution.py:40
  102.4 10.5 %collective-permute-start.13 = (f32[320,128]{1,0:T(8,128)}, f32[320,128]{1,0:T(8,128)S(1)}, u32[]{:S(2)}, u32[]{:S(2)}) collective-permute-start(f32[320,128]{1,0:T(8,128)} %get-tuple-element.75), channel_id=1, source_target_pairs={{0,24},{8,0},{16,8},{24,16},{1,25},{9,1},{17,9},{25,17},{2,26},{10... | collective-permute-start | bytes 491528 | tf_op jit(solution)/shard_map/ppermute | solution.py:40
  105.0 13.2 %all-to-all-start.1 = ((f32[32,4,128]{2,1,0:T(4,128)}), f32[32,4,128]{2,1,0:T(4,128)S(1)}, u32[]{:S(2)}, u32[]{:S(2)}) async-start(f32[32,4,128]{2,1,0:T(4,128)} %bitcast.15), calls=%async_computation.1 | async-start | bytes 131072 | tf_op jit(solution)/shard_map/all_to_all | solution.py:439
  110.1 2.8 %copy-start.5 = (f32[320,128]{1,0:T(8,128)}, f32[320,128]{1,0:T(8,128)S(1)}, u32[]{:S(2)}) copy-start(f32[320,128]{1,0:T(8,128)S(1)} %collective-permute-done.12.refs_3_) | copy-start | bytes 491524
  112.9 0.7 copy-start.7
  116.7 4.9 %collective-permute-start.14 = (f32[8,2560]{1,0:T(8,128)}, f32[8,2560]{1,0:T(8,128)S(1)}, u32[]{:S(2)}, u32[]{:S(2)}) collective-permute-start(f32[8,2560]{1,0:T(8,128)} %get-tuple-element.79), channel_id=1, source_target_pairs={{0,1},{1,0},{2,3},{3,2},{4,5},{5,4},{6,7},{7,6},{8,9},{9,8},{10,11... | collective-permute-start | bytes 245768 | tf_op jit(solution)/shard_map/ppermute | solution.py:40
  118.2 3.3 %copy-start = (f32[32,4,128]{2,1,0:T(4,128)}, f32[32,4,128]{2,1,0:T(4,128)S(1)}, u32[]{:S(2)}) copy-start(f32[32,4,128]{2,1,0:T(4,128)S(1)} %all-to-all-done.1) | copy-start | bytes 196612
  (2 other events, 1.2 us)

commit v2 on v1

--- a/solution.py
+++ b/solution.py
@@ -12,6 +12,7 @@
 HALO_LEVELS = 3
 AXES = ("gx", "gy", "gz")
 F32 = jnp.float32
+UNROLL = 24 * 24 * 128
 HI = lax.Precision.HIGHEST
 
 
@@ -21,6 +22,32 @@
 
 def dot(a, b, dims=((1,), (0,))):
     return lax.dot_general(a, b, (dims, ((), ())), precision=HI, preferred_element_type=F32)
+
+
+def halves(x):
+    high = x.astype(jnp.bfloat16).astype(F32)
+    return high, x - high
+
+
+def dot_right(x, hot):
+    both = jnp.concatenate(halves(x), axis=1).astype(jnp.bfloat16)
+    return lax.dot_general(
+        both, jnp.concatenate([hot, hot], axis=0).astype(jnp.bfloat16), (((1,), (0,)), ((), ())), preferred_element_type=F32
+    )
+
+
+def dot_pick(hot, x):
+    both = jnp.concatenate(halves(x), axis=1).astype(jnp.bfloat16)
+    return lax.dot_general(
+        jnp.concatenate([hot, hot], axis=1).astype(jnp.bfloat16), both, (((1,), (1,)), ((), ())), preferred_element_type=F32
+    )
+
+
+def dot_place(x, hot):
+    both = jnp.concatenate(halves(x), axis=0).astype(jnp.bfloat16)
+    return lax.dot_general(
+        both, jnp.concatenate([hot, hot], axis=0).astype(jnp.bfloat16), (((0,), (0,)), ((), ())), preferred_element_type=F32
+    )
 
 
 def iota(shape, dim):
@@ -57,42 +84,36 @@
         self.devices = counts[0] * counts[1] * counts[2]
         self.chunk = self.own[HALO_LEVELS][1]
         self.ext = [(n[0] + 2 * M, n[1] + 2 * M) for n in self.own[:HALO_LEVELS]]
+        self.tmp = pltpu.VMEM(
+            (max(r[0] for r in self.ring), max(r[1] for r in self.ring), 128), F32
+        )
         self.yrows = sum(n[0] * M for n in self.own[:HALO_LEVELS])
         self.xrows = sum(M * e[1] for e in self.ext)
         self.hcols = [up_to(e[0] * e[1], 128) for e in self.ext]
 
 
-def restrict_to(plan, level, source, store):
+def restrict_to(plan, level, source, tmp):
     nx, ny, nz = plan.own[level]
     lanes = plan.lanes
-    rz = one((iota((lanes, lanes), 0) >> 1 == iota((lanes, lanes), 1)) & (iota((lanes, lanes), 0) < nz))
-    ry = one(iota((ny // 2, ny), 1) >> 1 == iota((ny // 2, ny), 0)) * 0.125
-    pairs = jnp.sum(source[...].reshape(nx // 2, 2, ny, lanes), axis=1)
-    across = dot(pairs.reshape(nx // 2 * ny, lanes), rz).reshape(nx // 2, ny, lanes)
-    for i in range(nx // 2):
-        store(i, dot(ry, across[i]))
-
-
-def send_pack(plan, v, g1, g2, yl, yu, chunk, sums):
-    lanes = plan.lanes
-
-    def store1(i, u):
-        g1[i] = u
-
-    def store2(i, u):
-        g2[i] = u
-
-    restrict_to(plan, 0, v, store1)
-    restrict_to(plan, 1, g1, store2)
+    rz = one((iota((lanes, lanes), 0) >> 1 == iota((lanes, lanes), 1)) & (iota((lanes, lanes), 0) < nz)) * 0.125
+    hx, hy = nx // 2, ny // 2
+    for i in range(hx):
+        tmp[i, 0:ny, 0:lanes] = source[2 * i] + source[2 * i + 1]
+    pairs = tmp[0:hx, pl.ds(0, hy, stride=2), 0:lanes] + tmp[0:hx, pl.ds(1, hy, stride=2), 0:lanes]
+    if hy % 8:
+        return jnp.stack([dot_right(pairs[i], rz) for i in range(hx)])
+    return dot_right(pairs.reshape(hx * hy, lanes), rz).reshape(hx, hy, lanes)
+
+
+def send_pack(plan, v, g1, g2, yl, yu, chunk, sums, tmp):
+    lanes = plan.lanes
+    g1[...] = restrict_to(plan, 0, v, tmp)
+    g2[...] = restrict_to(plan, 1, g1, tmp)
     n3 = plan.own[3]
+    coarse = restrict_to(plan, 2, g2, tmp)
     parts = [jnp.zeros((n3[1], lanes), F32)]
-
-    def store3(i, u):
-        place = one(iota((lanes, lanes), 1) == iota((lanes, lanes), 0) + i * n3[2])
-        place = jnp.where(iota((lanes, lanes), 0) < n3[2], place, 0.0)
-        parts[0] = parts[0] + dot(u, place)
-
-    restrict_to(plan, 2, g2, store3)
+    for i in range(n3[0]):
+        parts[0] = parts[0] + (pltpu.roll(coarse[i], i * n3[2], 1) if i else coarse[i])
     payload = parts[0]
     if sums is not None:
         at = iota(payload.shape, 1)
@@ -134,17 +155,28 @@
     source, target = g, a
     for sweep in range(SWEEPS - 1):
 
-        def body(i, carry, source=source, target=target):
+        group = rx if rx * ry * rz <= UNROLL else max(u for u in range(1, 9) if rx % u == 0)
+
+        def plane(i, source=source, target=target):
+            fixed = isinstance(i, int)
             f = source[i]
-            before = source[jnp.where(i == 0, rx - 1, i - 1)]
-            after = source[jnp.where(i == rx - 1, 0, i + 1)]
+            before = source[(i - 1) % rx if fixed else jnp.where(i == 0, rx - 1, i - 1)]
+            after = source[(i + 1) % rx if fixed else jnp.where(i == rx - 1, 0, i + 1)]
             beside = before + after + pltpu.roll(f, 1, 0) + pltpu.roll(f, ry - 1, 0)
             beside = beside + pltpu.roll(f, 1, 1) + pltpu.roll(f, rz - 1, 1)
-            sx = one(inside(plan, idx, level, 0, i))
+            sx = one(inside(plan, idx, level, 0, jnp.int32(i)))
             target[i] = g[i] + (m9 * sx) * (3.0 * f + beside)
+
+        def body(j, carry, plane=plane, group=group):
+            for u in range(group):
+                plane(j * group + u)
             return carry
 
-        lax.fori_loop(0, rx, body, 0)
+        if group == rx:
+            for i in range(rx):
+                plane(i)
+        else:
+            lax.fori_loop(0, rx // group, body, 0)
         source, target = target, (b if target is a else a)
     return source
 
@@ -160,30 +192,36 @@
     return (fine >> 1 == coarse) & (fine < plan.whole[level][dim])
 
 
-def add_prolonged(plan, idx, level, f, scale, zc, out):
+def add_prolonged(plan, idx, level, f, scale, zc, out, tmp):
     rx, ry, rz = plan.ring[level]
     cx, cy, cz = plan.ring[level + 1]
     pz = one(coarse_map(plan, idx, level, 2, iota((cz, rz), 1), iota((cz, rz), 0)))
-    py = one(coarse_map(plan, idx, level, 1, iota((ry, cy), 0), iota((ry, cy), 1)))
     halo = level < HALO_LEVELS
     low = -1 if halo else 0
     high = plan.own[level][0] + 1 if halo else plan.whole[level][0]
+    planes = range(low >> 1, (high - 1 >> 1) + 1)
     if level + 1 == HALO_LEVELS:
-        for s in range(low, high):
-            i = s % rx
-            at = s + idx[0] * plan.own[level][0]
-            ok = (at >= 0) & (at < plan.whole[level][0])
-            c = jnp.clip(at >> 1, 0, plan.whole[level + 1][0] - 1)
-            u = dot(py, dot(zc[c], pz))
-            out[i] = scale * f[i] + one(ok) * u
+        py = one(coarse_map(plan, idx, level, 1, iota((ry, cy), 0), iota((ry, cy), 1)))
+        for k in planes:
+            at = k + idx[0] * (plan.own[level][0] // 2)
+            ok = (at >= 0) & (at < plan.whole[level + 1][0])
+            c = jnp.clip(at, 0, plan.whole[level + 1][0] - 1)
+            u = dot(py, dot_right(zc[c], pz)) * one(ok)
+            for s in (2 * k, 2 * k + 1):
+                if low <= s < high:
+                    out[s % rx] = scale * f[s % rx] + u
         return
-    spread = dot(zc[...].reshape(cx * cy, cz), pz).reshape(cx, cy, rz)
-    for c in range(low >> 1, (high - 1 >> 1) + 1):
-        u = dot(py, spread[c % cx])
-        for s in (2 * c, 2 * c + 1):
+    upper = (plan.own[level][1] + M) // 2 if halo else ry // 2
+    for n, k in enumerate(planes):
+        for odd in (0, 1):
+            tmp[n, pl.ds(odd, upper, stride=2), 0:cz] = zc[k % cx, 0:upper, :]
+            if halo:
+                tmp[n, pl.ds(2 * upper + odd, M // 2, stride=2), 0:cz] = zc[k % cx, cy - M // 2 : cy, :]
+    spread = dot_right(tmp[0 : len(planes), 0:ry, 0:cz].reshape(len(planes) * ry, cz), pz).reshape(len(planes), ry, rz)
+    for n, k in enumerate(planes):
+        for s in (2 * k, 2 * k + 1):
             if low <= s < high:
-                i = s % rx
-                out[i] = scale * f[i] + u
+                out[s % rx] = scale * f[s % rx] + spread[n]
     if not halo:
         for i in range(high, rx):
             out[i] = jnp.zeros((ry, rz), F32)
@@ -198,10 +236,10 @@
     yu[...] = guess[:, ny - 1, :]
     at, row = iota((8, lanes), 1), iota((8, lanes), 0)
     pick = one(((row == 0) & (at == 0)) | ((row == 1) & (at == nz - 1)))
-    zf[...] = dot(pick, guess[...].reshape(nx * ny, lanes), ((1,), (1,)))
-
-
-def residual_kernel(plan, idx, b, guess, xlo, xhi, ylo, yhi, zlo, zhi, r, g1, g2, yl, yu, chunk, side):
+    zf[...] = dot_pick(pick, guess[...].reshape(nx * ny, lanes))
+
+
+def residual_kernel(plan, idx, b, guess, xlo, xhi, ylo, yhi, zlo, zhi, r, g1, g2, yl, yu, chunk, side, tmp):
     nx, ny, nz = plan.local
     lanes = plan.lanes
     cx, cy, cz = plan.counts
@@ -209,7 +247,8 @@
     at, row = iota((8, lanes), 1), iota((8, lanes), 0)
     upper = one((row == 0) & (at == nz - 1)) * has(2, True)
     lower = one((row == 1) & (at == 0)) * has(2, False)
-    side[...] = (dot(zhi[...], upper, ((0,), (0,))) + dot(zlo[...], lower, ((0,), (0,)))).reshape(nx, ny, lanes)
+    got = jnp.where(iota((8, nx * ny), 0) == 0, zhi[...], zlo[...])
+    side[...] = dot_place(got, upper + lower).reshape(nx, ny, lanes)
     ys, zs = iota((ny, lanes), 0), iota((ny, lanes), 1)
     not_low, not_high = one(zs > 0), one(zs < nz - 1)
     y_low, y_high = ys == 0, ys == ny - 1
@@ -222,7 +261,7 @@
         beside = beside + jnp.where(y_high, (yhi[i] * has(1, True))[None, :], pltpu.roll(f, ny - 1, 0))
         beside = beside + pltpu.roll(f, 1, 1) * not_low + pltpu.roll(f, lanes - 1, 1) * not_high
         r[i] = b[i] - (6.0 * f - (beside + side[i]))
-    send_pack(plan, r, g1, g2, yl, yu, chunk, None)
+    send_pack(plan, r, g1, g2, yl, yu, chunk, None, tmp)
 
 
 def ring_y_kernel(plan, v, g1, g2, ylo, yhi, a0, a1, a2, xl, xu):
@@ -254,7 +293,7 @@
             c[nx + M + i] = xlo[row : row + e, :]
             row += e
         pick = one(at == jnp.where(k < M, k, nz - 2 * M + k))
-        h[:, col : col + ex * e] = dot(pick, c[...].reshape(ex * e, lanes), ((1,), (1,)))
+        h[:, col : col + ex * e] = dot_pick(pick, c[...].reshape(ex * e, lanes))
         if plan.hcols[l] > ex * e:
             h[:, col + ex * e : col + plan.hcols[l]] = jnp.zeros((8, plan.hcols[l] - ex * e), F32)
         col += plan.hcols[l]
@@ -285,7 +324,7 @@
         rings = outs[7:11]
         scratch = outs[11:]
     bufs = [scratch[2 * l : 2 * l + 2] for l in range(LEVELS)]
-    g4, g5 = scratch[2 * LEVELS : 2 * LEVELS + 2]
+    g4, g5, tmp = scratch[2 * LEVELS : 2 * LEVELS + 3]
     fields = list(rings) + [g4, g5]
     lanes = plan.lanes
     if last:
@@ -303,7 +342,7 @@
         place = one(at == want)
         got = jnp.where(iota((8, ex * e), 0) < M, hhi[:, col : col + ex * e], hlo[:, col : col + ex * e])
         col += plan.hcols[l]
-        tile = dot(got, place, ((0,), (0,))).reshape(ex, e, lanes)
+        tile = dot_place(got, place).reshape(ex, e, lanes)
         for i in range(rx):
             m = mask * one(inside(plan, idx, l, 0, jnp.int32(i)))
             if base:
@@ -330,11 +369,18 @@
     for l in (3, 4):
         rx, ry, rz = plan.ring[l]
         cx, cy, cz = plan.ring[l + 1]
-        rzm = one((iota((rz, cz), 0) >> 1 == iota((rz, cz), 1)) & (iota((rz, cz), 0) < plan.whole[l][2]))
-        rym = one((iota((cy, ry), 1) >> 1 == iota((cy, ry), 0)) & (iota((cy, ry), 1) < plan.whole[l][1])) * 0.125
-        for i in range(plan.whole[l + 1][0]):
-            fields[l + 1][i] = dot(rym, dot(fields[l][2 * i] + fields[l][2 * i + 1], rzm))
-        fields[l + 1][cx - 1] = jnp.zeros((cy, cz), F32)
+        rzm = one((iota((rz, cz), 0) >> 1 == iota((rz, cz), 1)) & (iota((rz, cz), 0) < plan.whole[l][2])) * 0.125
+        hx, hy = plan.whole[l + 1][:2]
+        fields[l + 1][...] = jnp.zeros((cx, cy, cz), F32)
+        for i in range(hx):
+            both = fields[l][2 * i] + fields[l][2 * i + 1]
+            pieces = []
+            for t in range(0, rz, 128):
+                n = i * (rz // 128) + t // 128
+                tmp[n, 0:ry, :] = both[:, t : t + 128]
+                pieces.append(tmp[n, pl.ds(0, ry // 2, stride=2), :] + tmp[n, pl.ds(1, ry // 2, stride=2), :])
+            pair = jnp.concatenate(pieces, axis=1)
+            fields[l + 1][i, 0 : ry // 2, :] = dot_right(pair, rzm)
     zc = None
     for l in range(LEVELS - 1, -1, -1):
         f = smooth(plan, idx, l, fields[l], *bufs[l])
@@ -343,33 +389,39 @@
         if zc is None:
             out[...] = scale * f[...]
         else:
-            add_prolonged(plan, idx, l, f, scale, zc, out)
+            add_prolonged(plan, idx, l, f, scale, zc, out, tmp)
         zc = out
     nx, ny, nz = plan.local
     rx, ry, rz = plan.ring[0]
     first = jnp.zeros((ny, lanes), F32)
     second = jnp.zeros((ny, lanes), F32)
 
-    def body(i, carry):
+    group = max(u for u in range(1, 5) if nx % u == 0)
+
+    def body(j, carry):
         first, second = carry
-        f = zc[i]
-        before = zc[jnp.where(i == 0, rx - 1, i - 1)]
-        after = zc[i + 1]
-        beside = before + after + pltpu.roll(f, 1, 0) + pltpu.roll(f, ry - 1, 0)
-        beside = beside + pltpu.roll(f, 1, 1) + pltpu.roll(f, rz - 1, 1)
-        w = (6.0 * f - beside)[:ny, :lanes]
-        z = f[:ny, :lanes]
-        z_out[i] = z
-        w_out[i] = w
-        return first + z * rings[0][i][:ny, :lanes], second + z * w
-
-    first, second = lax.fori_loop(0, nx, body, (first, second))
+        for u in range(group):
+            i = j * group + u
+            f = zc[i]
+            before = zc[jnp.where(i == 0, rx - 1, i - 1)]
+            after = zc[i + 1]
+            beside = before + after + pltpu.roll(f, 1, 0) + pltpu.roll(f, ry - 1, 0)
+            beside = beside + pltpu.roll(f, 1, 1) + pltpu.roll(f, rz - 1, 1)
+            w = (6.0 * f - beside)[:ny, :lanes]
+            z = f[:ny, :lanes]
+            z_out[i] = z
+            w_out[i] = w
+            first = first + z * rings[0][i][:ny, :lanes]
+            second = second + z * w
+        return first, second
+
+    first, second = lax.fori_loop(0, nx // group, body, (first, second))
     sums = (jnp.sum(first), jnp.sum(second))
     if last:
         row, at = iota(sums_out.shape, 0), iota(sums_out.shape, 1)
         sums_out[...] = jnp.where(at == lanes - 2, sums[0], jnp.where(at == lanes - 1, sums[1], 0.0))
     else:
-        send_pack(plan, w_out, g1, g2, yl, yu, chunk, sums)
+        send_pack(plan, w_out, g1, g2, yl, yu, chunk, sums, tmp)
 
 
 def final_kernel(plan, chunks1, chunks2, guess, r, z1, w1, z2, w2, x_out, r_out):
@@ -425,13 +477,13 @@
         bind(residual_kernel),
         [own[0]] + packs,
         [idx, right_side, guess, xlo, xhi, ylo, yhi, zlo, zhi],
-        [pltpu.VMEM((nx, ny, lanes), F32)],
+        [pltpu.VMEM((nx, ny, lanes), F32), plan.tmp],
         smem=True,
     )
     rings = [sds(*s) for s in plan.ring[:4]]
     as_scratch = lambda items: [pltpu.VMEM(s.shape, F32) for s in items]
     work = [pltpu.VMEM(s, F32) for s in plan.ring for _ in range(2)]
-    work += [pltpu.VMEM(s, F32) for s in plan.ring[4:6]]
+    work += [pltpu.VMEM(s, F32) for s in plan.ring[4:6]] + [plan.tmp]
     field, old = r, []
     kept = []
     for step in range(STEPS):

time: 181 us -> 109 us (0.60)
  Pallas kernels: 111 us -> 39.3 us
    pallas_call x9, Pallas kernels: 111 us -> 39.3 us  [call(): pl.pallas_call(body, out_shape=tuple(outs), in_specs=specs, out_specs=tup...]
  transfers between devices with their start and end apart: 17 -> 17, of which waited for: 11 -> 12; matrix products, arithmetic and copies ran while one was open for 0% -> 1% of each run, Pallas kernels for 3% -> 5%
where the time goes in v2:
time: 109 us
  Pallas kernels  39.3 us (36%)
  starting transfers between devices  28.5 us (26%)
  waiting for transfers between devices  23.6 us (22%)
  blocking collectives  11.5 us (11%)
  local copies, waits for them, and re-layouts  4.46 us (4%)
    pallas_call x9, Pallas kernels, call(): pl.pallas_call(body, out_shape=tuple(outs), in_specs=specs, out_specs=tup...  39.3 us
    ppermute x15, waiting for transfers between devices, cyclic(): lax.ppermute(value, axis, [(i, (i + by) % count) for i in range(count)])  23.5 us
    ppermute x15, starting transfers between devices, cyclic(): lax.ppermute(value, axis, [(i, (i + by) % count) for i in range(count)])  22.7 us
    all_to_all x1, blocking collectives, shards(): sums = lax.all_to_all(sums, AXES, 0, 0, tiled=True)  11.5 us
    all_to_all x2, starting transfers between devices, shards(): chunks = lax.all_to_all(chunk, AXES, 0, 0, tiled=True)  5.77 us
    unnamed x34, local copies, waits for them, and re-layouts  4.46 us
  transfers between devices with their start and end apart: 17, of which 12 were waited for; matrix products, arithmetic and copies ran while one was open for 1% of the time, Pallas kernels for 5%

profile of v2, /device:TPU:0, one launch (start us, length us, event | category | flops | bytes accessed | tf_op | source)
XLA Modules:
  0.0 108.7 jit_solution(9012750728069472916)
XLA Ops:
  0.6 1.9 %shard_map.41 = (f32[32,128]{1,0:T(8,128)}, f32[32,128]{1,0:T(8,128)}, f32[32,128]{1,0:T(8,128)}, f32[32,128]{1,0:T(8,128)}, f32[8,1024]{1,0:T(8,128)}) custom-call(f32[32,32,128]{2,1,0:T(8,128)} %refs_2_.3), custom_call_target="tpu_custom_call" | custom-call | tf_op jit(solution)/shard_map/pallas_call | solution.py:447
  2.5 3.1 %collective-permute-start = (f32[32,128]{1,0:T(8,128)}, f32[32,128]{1,0:T(8,128)S(1)}, u32[]{:S(2)}, u32[]{:S(2)}) collective-permute-start(f32[32,128]{1,0:T(8,128)} %get-tuple-element.45), channel_id=1, source_target_pairs={{0,8},{8,16},{16,24},{24,0},{1,9},{9,17},{17,25},{25,1},{2,10},{10... | collective-permute-start | bytes 49160 | tf_op jit(solution)/shard_map/ppermute | solution.py:67
  5.6 2.0 %collective-permute-start.1 = (f32[32,128]{1,0:T(8,128)}, f32[32,128]{1,0:T(8,128)S(1)}, u32[]{:S(2)}, u32[]{:S(2)}) collective-permute-start(f32[32,128]{1,0:T(8,128)} %get-tuple-element.46), channel_id=1, source_target_pairs={{0,24},{8,0},{16,8},{24,16},{1,25},{9,1},{17,9},{25,17},{2,26},{10... | collective-permute-start | bytes 49160 | tf_op jit(solution)/shard_map/ppermute | solution.py:67
  7.6 1.7 %collective-permute-start.3 = (f32[32,128]{1,0:T(8,128)}, f32[32,128]{1,0:T(8,128)S(1)}, u32[]{:S(2)}, u32[]{:S(2)}) collective-permute-start(f32[32,128]{1,0:T(8,128)} %get-tuple-element.48), channel_id=1, source_target_pairs={{0,6},{2,0},{4,2},{6,4},{1,7},{3,1},{5,3},{7,5},{8,14},{10,8},{12,... | collective-permute-start | bytes 49160 | tf_op jit(solution)/shard_map/ppermute | solution.py:67
  9.4 1.7 %collective-permute-start.4 = (f32[8,1024]{1,0:T(8,128)}, f32[8,1024]{1,0:T(8,128)S(1)}, u32[]{:S(2)}, u32[]{:S(2)}) collective-permute-start(f32[8,1024]{1,0:T(8,128)} %get-tuple-element.49), channel_id=1, source_target_pairs={{0,1},{1,0},{2,3},{3,2},{4,5},{5,4},{6,7},{7,6},{8,9},{9,8},{10,11... | collective-permute-start | bytes 98312 | tf_op jit(solution)/shard_map/ppermute | solution.py:67
  11.7 1.8 %collective-permute-done.4.refs_7_.refs_8_ = f32[8,1024]{1,0:T(8,128)S(1)} collective-permute-done((f32[8,1024]{1,0:T(8,128)}, f32[8,1024]{1,0:T(8,128)S(1)}, u32[]{:S(2)}, u32[]{:S(2)}) %collective-permute-start.4) | collective-permute-done | bytes 32800 | tf_op jit(solution)/shard_map/ppermute | solution.py:67
  14.1 2.9 %shard_map.42 = (f32[32,32,128]{2,1,0:T(8,128)}, f32[16,16,128]{2,1,0:T(8,128)}, f32[8,8,128]{2,1,0:T(8,128)}, f32[224,128]{1,0:T(8,128)}, f32[224,128]{1,0:T(8,128)}, /*index=5*/f32[128,128]{1,0:T(8,128)}) custom-call(s32[3]{0:T(128)} %pad_add_fusion.refs_0_, f32[32,32,128]{2,1,0:T(8,128)} %refs_1_.1, f32[32,32,128]{2,1,0:T(8,128)} %refs_2_.3, ...), custom_call_target="tpu_custom_call" | custom-call | tf_op jit(solution)/shard_map/pallas_call | solution.py:447
  17.0 1.7 %collective-permute-start.6 = (f32[224,128]{1,0:T(8,128)}, f32[224,128]{1,0:T(8,128)S(1)}, u32[]{:S(2)}, u32[]{:S(2)}) collective-permute-start(f32[224,128]{1,0:T(8,128)} %get-tuple-element.54), channel_id=1, source_target_pairs={{0,6},{2,0},{4,2},{6,4},{1,7},{3,1},{5,3},{7,5},{8,14},{10,8},{12,... | collective-permute-start | bytes 344072 | tf_op jit(solution)/shard_map/ppermute | solution.py:67
  18.7 2.7 %collective-permute-done.5.refs_3_ = f32[224,128]{1,0:T(8,128)S(1)} collective-permute-done((f32[224,128]{1,0:T(8,128)}, f32[224,128]{1,0:T(8,128)S(1)}, u32[]{:S(2)}, u32[]{:S(2)}) %collective-permute-start.5) | collective-permute-done | bytes 114720 | tf_op jit(solution)/shard_map/ppermute | solution.py:67
  22.7 2.2 %shard_map.43 = (f32[32,40,128]{2,1,0:T(8,128)}, f32[16,24,128]{2,1,0:T(8,128)}, f32[8,16,128]{2,1,0:T(8,128)}, f32[320,128]{1,0:T(8,128)}, f32[320,128]{1,0:T(8,128)}) custom-call(f32[32,32,128]{2,1,0:T(8,128)} %get-tuple-element.50.refs_0_.refs_3_, f32[16,16,128]{2,1,0:T(8,128)} %get-tuple-element.51.refs_1_, f32[8,8,128]{2,1,0:T(8,128)} %get-tuple-element.52.refs_2_, ...), custom_call_target="tpu_custom_call" | custom-call | tf_op jit(solution)/shard_map/pallas_call | solution.py:447
  24.9 3.8 %collective-permute-start.8 = (f32[320,128]{1,0:T(8,128)}, f32[320,128]{1,0:T(8,128)S(1)}, u32[]{:S(2)}, u32[]{:S(2)}) collective-permute-start(f32[320,128]{1,0:T(8,128)} %get-tuple-element.59), channel_id=1, source_target_pairs={{0,24},{8,0},{16,8},{24,16},{1,25},{9,1},{17,9},{25,17},{2,26},{10... | collective-permute-start | bytes 491528 | tf_op jit(solution)/shard_map/ppermute | solution.py:67
  28.7 2.9 %all-to-all-start = ((f32[32,4,128]{2,1,0:T(4,128)}), f32[32,4,128]{2,1,0:T(4,128)S(1)}, u32[]{:S(2)}, u32[]{:S(2)}) async-start(f32[32,4,128]{2,1,0:T(4,128)} %bitcast.16), calls=%async_computation | async-start | bytes 131072 | tf_op jit(solution)/shard_map/all_to_all | solution.py:491
  31.7 2.1 %collective-permute-done.7.refs_3_ = f32[320,128]{1,0:T(8,128)S(1)} collective-permute-done((f32[320,128]{1,0:T(8,128)}, f32[320,128]{1,0:T(8,128)S(1)}, u32[]{:S(2)}, u32[]{:S(2)}) %collective-permute-start.7) | collective-permute-done | bytes 163872 | tf_op jit(solution)/shard_map/ppermute | solution.py:67
  33.8 1.6 %collective-permute-done.8.refs_4_ = f32[320,128]{1,0:T(8,128)S(1)} collective-permute-done((f32[320,128]{1,0:T(8,128)}, f32[320,128]{1,0:T(8,128)S(1)}, u32[]{:S(2)}, u32[]{:S(2)}) %collective-permute-start.8) | collective-permute-done | bytes 163872 | tf_op jit(solution)/shard_map/ppermute | solution.py:67
  36.1 2.5 %shard_map.44 = (f32[40,40,128]{2,1,0:T(8,128)}, f32[24,24,128]{2,1,0:T(8,128)}, f32[16,16,128]{2,1,0:T(8,128)}, f32[8,2560]{1,0:T(8,128)}) custom-call(f32[32,40,128]{2,1,0:T(8,128)} %get-tuple-element.55.refs_0_, f32[16,24,128]{2,1,0:T(8,128)} %get-tuple-element.56.refs_1_, f32[8,16,128]{2,1,0:T(8,128)} %get-tuple-element.57.refs_2_, ...), custom_call_target="tpu_custom_call" | custom-call | tf_op jit(solution)/shard_map/pallas_call | solution.py:447
  38.6 1.5 %collective-permute-start.9 = (f32[8,2560]{1,0:T(8,128)}, f32[8,2560]{1,0:T(8,128)S(1)}, u32[]{:S(2)}, u32[]{:S(2)}) collective-permute-start(f32[8,2560]{1,0:T(8,128)} %get-tuple-element.63), channel_id=1, source_target_pairs={{0,1},{1,0},{2,3},{3,2},{4,5},{5,4},{6,7},{7,6},{8,9},{9,8},{10,11... | collective-permute-start | bytes 245768 | tf_op jit(solution)/shard_map/ppermute | solution.py:67
  40.2 3.6 %collective-permute-done.9.refs_4_.refs_5_ = f32[8,2560]{1,0:T(8,128)S(1)} collective-permute-done((f32[8,2560]{1,0:T(8,128)}, f32[8,2560]{1,0:T(8,128)S(1)}, u32[]{:S(2)}, u32[]{:S(2)}) %collective-permute-start.9) | collective-permute-done | bytes 81952 | tf_op jit(solution)/shard_map/ppermute | solution.py:67
  44.4 11.0 %shard_map.45 = (f32[32,32,128]{2,1,0:T(8,128)}, f32[32,32,128]{2,1,0:T(8,128)}, f32[16,16,128]{2,1,0:T(8,128)}, f32[8,8,128]{2,1,0:T(8,128)}, f32[224,128]{1,0:...) custom-call(s32[3]{0:T(128)} %pad_add_fusion.refs_0_, ...), custom_call_target="tpu_custom_call" | custom-call | tf_op jit(solution)/shard_map/pallas_call | solution.py:447
  55.4 1.7 %collective-permute-start.11 = (f32[224,128]{1,0:T(8,128)}, f32[224,128]{1,0:T(8,128)S(1)}, u32[]{:S(2)}, u32[]{:S(2)}) collective-permute-start(f32[224,128]{1,0:T(8,128)} %get-tuple-element.70), channel_id=1, source_target_pairs={{0,6},{2,0},{4,2},{6,4},{1,7},{3,1},{5,3},{7,5},{8,14},{10,8},{12,... | collective-permute-start | bytes 344072 | tf_op jit(solution)/shard_map/ppermute | solution.py:67
  57.1 2.7 %collective-permute-done.10.refs_3_ = f32[224,128]{1,0:T(8,128)S(1)} collective-permute-done((f32[224,128]{1,0:T(8,128)}, f32[224,128]{1,0:T(8,128)S(1)}, u32[]{:S(2)}, u32[]{:S(2)}) %collective-permute-start.10) | collective-permute-done | bytes 114720 | tf_op jit(solution)/shard_map/ppermute | solution.py:67
  60.6 2.2 %shard_map.46 = (f32[32,40,128]{2,1,0:T(8,128)}, f32[16,24,128]{2,1,0:T(8,128)}, f32[8,16,128]{2,1,0:T(8,128)}, f32[320,128]{1,0:T(8,128)}, f32[320,128]{1,0:T(8,128)}) custom-call(f32[32,32,128]{2,1,0:T(8,128)} %get-tuple-element.66.refs_0_.refs_5_, f32[16,16,128]{2,1,0:T(8,128)} %get-tuple-element.67.refs_1_, f32[8,8,128]{2,1,0:T(8,128)} %get-tuple-element.68.refs_2_, ...), custom_call_target="tpu_custom_call" | custom-call | tf_op jit(solution)/shard_map/pallas_call | solution.py:447
  62.8 1.2 %collective-permute-start.12 = (f32[320,128]{1,0:T(8,128)}, f32[320,128]{1,0:T(8,128)S(1)}, u32[]{:S(2)}, u32[]{:S(2)}) collective-permute-start(f32[320,128]{1,0:T(8,128)} %get-tuple-element.74), channel_id=1, source_target_pairs={{0,8},{8,16},{16,24},{24,0},{1,9},{9,17},{17,25},{25,1},{2,10},{10... | collective-permute-start | bytes 491528 | tf_op jit(solution)/shard_map/ppermute | solution.py:67
  64.0 2.7 %collective-permute-start.13 = (f32[320,128]{1,0:T(8,128)}, f32[320,128]{1,0:T(8,128)S(1)}, u32[]{:S(2)}, u32[]{:S(2)}) collective-permute-start(f32[320,128]{1,0:T(8,128)} %get-tuple-element.75), channel_id=1, source_target_pairs={{0,24},{8,0},{16,8},{24,16},{1,25},{9,1},{17,9},{25,17},{2,26},{10... | collective-permute-start | bytes 491528 | tf_op jit(solution)/shard_map/ppermute | solution.py:67
  66.6 2.9 %all-to-all-start.1 = ((f32[32,4,128]{2,1,0:T(4,128)}), f32[32,4,128]{2,1,0:T(4,128)S(1)}, u32[]{:S(2)}, u32[]{:S(2)}) async-start(f32[32,4,128]{2,1,0:T(4,128)} %bitcast.15), calls=%async_computation.1 | async-start | bytes 131072 | tf_op jit(solution)/shard_map/all_to_all | solution.py:491
  69.5 2.2 %collective-permute-done.12.refs_3_ = f32[320,128]{1,0:T(8,128)S(1)} collective-permute-done((f32[320,128]{1,0:T(8,128)}, f32[320,128]{1,0:T(8,128)S(1)}, u32[]{:S(2)}, u32[]{:S(2)}) %collective-permute-start.12) | collective-permute-done | bytes 163872 | tf_op jit(solution)/shard_map/ppermute | solution.py:67
  71.7 2.8 %collective-permute-done.13.refs_4_ = f32[320,128]{1,0:T(8,128)S(1)} collective-permute-done((f32[320,128]{1,0:T(8,128)}, f32[320,128]{1,0:T(8,128)S(1)}, u32[]{:S(2)}, u32[]{:S(2)}) %collective-permute-start.13) | collective-permute-done | bytes 163872 | tf_op jit(solution)/shard_map/ppermute | solution.py:67
  75.2 2.6 %shard_map.47 = (f32[40,40,128]{2,1,0:T(8,128)}, f32[24,24,128]{2,1,0:T(8,128)}, f32[16,16,128]{2,1,0:T(8,128)}, f32[8,2560]{1,0:T(8,128)}) custom-call(f32[32,40,128]{2,1,0:T(8,128)} %get-tuple-element.71.refs_0_, f32[16,24,128]{2,1,0:T(8,128)} %get-tuple-element.72.refs_1_, f32[8,16,128]{2,1,0:T(8,128)} %get-tuple-element.73.refs_2_, ...), custom_call_target="tpu_custom_call" | custom-call | tf_op jit(solution)/shard_map/pallas_call | solution.py:447
  77.8 1.5 %collective-permute-start.14 = (f32[8,2560]{1,0:T(8,128)}, f32[8,2560]{1,0:T(8,128)S(1)}, u32[]{:S(2)}, u32[]{:S(2)}) collective-permute-start(f32[8,2560]{1,0:T(8,128)} %get-tuple-element.79), channel_id=1, source_target_pairs={{0,1},{1,0},{2,3},{3,2},{4,5},{5,4},{6,7},{7,6},{8,9},{9,8},{10,11... | collective-permute-start | bytes 245768 | tf_op jit(solution)/shard_map/ppermute | solution.py:67
  79.3 3.3 %collective-permute-done.14.refs_4_.refs_5_ = f32[8,2560]{1,0:T(8,128)S(1)} collective-permute-done((f32[8,2560]{1,0:T(8,128)}, f32[8,2560]{1,0:T(8,128)S(1)}, u32[]{:S(2)}, u32[]{:S(2)}) %collective-permute-start.14) | collective-permute-done | bytes 81952 | tf_op jit(solution)/shard_map/ppermute | solution.py:67
  83.2 10.8 %shard_map.48 = (f32[32,32,128]{2,1,0:T(8,128)}, f32[32,32,128]{2,1,0:T(8,128)}, f32[32,128]{1,0:T(8,128)}) custom-call(s32[3]{0:T(128)} %pad_add_fusion.refs_0_, f32[40,40,128]{2,1,0:T(8,128)} %get-tuple-element.76.refs_1_, f32[24,24,128]{2,1,0:T(8,128)} %get-tuple-element.77.refs_2_, f32[16,16,128]{2,1,0:T(8,128)} %get-tuple-element.78.refs_3_, ...), custom_call_target="tpu_custom_call" | custom-call | tf_op jit(solution)/shard_map/pallas_call | solution.py:447
  94.0 11.5 %all_to_all.33 = f32[32,1,128]{2,1,0:T(1,128)} all-to-all(f32[32,1,128]{2,1,0:T(1,128)} %bitcast.17), channel_id=1, replica_groups=mesh['gx'=4,'gy'=4,'gz'=2] {'gx','gy','gz'}, dimensions={0} | all-to-all | bytes 32768 | tf_op jit(solution)/shard_map/all_to_all | solution.py:516
  105.5 3.2 %shard_map.49 = (f32[32,32,128]{2,1,0:T(8,128)}, f32[32,32,128]{2,1,0:T(8,128)}) custom-call(f32[128,128]{1,0:T(8,128)} %bitcast.12, f32[32,128]{1,0:T(8,128)} %bitcast.14, f32[32,32,128]{2,1,0:T(8,128)} %refs_2_.3, f32[32,32,128]{2,1,0:T(8,128)} %get-tuple-element.50.refs_0_.refs_3_, f32[32,32,128]{2,1,0:T(8,128)} %get-tuple-element.85.refs_4_, ...), custom_call_target="tpu_custom_call" | custom-call | tf_op jit(solution)/shard_map/pallas_call | solution.py:447
  (47 shorter events, 5.9 us)
Async XLA Ops:
  2.5 9.1 %collective-permute-start = (f32[32,128]{1,0:T(8,128)}, f32[32,128]{1,0:T(8,128)S(1)}, u32[]{:S(2)}, u32[]{:S(2)}) collective-permute-start(f32[32,128]{1,0:T(8,128)} %get-tuple-element.45), channel_id=1, source_target_pairs={{0,8},{8,16},{16,24},{24,0},{1,9},{9,17},{17,25},{25,1},{2,10},{10... | collective-permute-start | bytes 49160 | tf_op jit(solution)/shard_map/ppermute | solution.py:67
  5.6 6.1 %collective-permute-start.1 = (f32[32,128]{1,0:T(8,128)}, f32[32,128]{1,0:T(8,128)S(1)}, u32[]{:S(2)}, u32[]{:S(2)}) collective-permute-start(f32[32,128]{1,0:T(8,128)} %get-tuple-element.46), channel_id=1, source_target_pairs={{0,24},{8,0},{16,8},{24,16},{1,25},{9,1},{17,9},{25,17},{2,26},{10... | collective-permute-start | bytes 49160 | tf_op jit(solution)/shard_map/ppermute | solution.py:67
  7.6 4.1 %collective-permute-start.2 = (f32[32,128]{1,0:T(8,128)}, f32[32,128]{1,0:T(8,128)S(1)}, u32[]{:S(2)}, u32[]{:S(2)}) collective-permute-start(f32[32,128]{1,0:T(8,128)} %get-tuple-element.47), channel_id=1, source_target_pairs={{0,2},{2,4},{4,6},{6,0},{1,3},{3,5},{5,7},{7,1},{8,10},{10,12},{12... | collective-permute-start | bytes 49160 | tf_op jit(solution)/shard_map/ppermute | solution.py:67
  7.6 4.1 %collective-permute-start.3 = (f32[32,128]{1,0:T(8,128)}, f32[32,128]{1,0:T(8,128)S(1)}, u32[]{:S(2)}, u32[]{:S(2)}) collective-permute-start(f32[32,128]{1,0:T(8,128)} %get-tuple-element.48), channel_id=1, source_target_pairs={{0,6},{2,0},{4,2},{6,4},{1,7},{3,1},{5,3},{7,5},{8,14},{10,8},{12,... | collective-permute-start | bytes 49160 | tf_op jit(solution)/shard_map/ppermute | solution.py:67
  9.4 4.1 %collective-permute-start.4 = (f32[8,1024]{1,0:T(8,128)}, f32[8,1024]{1,0:T(8,128)S(1)}, u32[]{:S(2)}, u32[]{:S(2)}) collective-permute-start(f32[8,1024]{1,0:T(8,128)} %get-tuple-element.49), channel_id=1, source_target_pairs={{0,1},{1,0},{2,3},{3,2},{4,5},{5,4},{6,7},{7,6},{8,9},{9,8},{10,11... | collective-permute-start | bytes 98312 | tf_op jit(solution)/shard_map/ppermute | solution.py:67
  11.7 1.8 %copy-start.13 = (f32[32,128]{1,0:T(8,128)}, f32[32,128]{1,0:T(8,128)S(1)}, u32[]{:S(2)}) copy-start(f32[32,128]{1,0:T(8,128)S(1)} %collective-permute-done.refs_3_) | copy-start | bytes 49156
  11.7 1.8 %copy-start.14 = (f32[32,128]{1,0:T(8,128)}, f32[32,128]{1,0:T(8,128)S(1)}, u32[]{:S(2)}) copy-start(f32[32,128]{1,0:T(8,128)S(1)} %collective-permute-done.1.refs_4_) | copy-start | bytes 49156
  11.7 1.8 %copy-start.15 = (f32[32,128]{1,0:T(8,128)}, f32[32,128]{1,0:T(8,128)S(1)}, u32[]{:S(2)}) copy-start(f32[32,128]{1,0:T(8,128)S(1)} %collective-permute-done.2.refs_5_) | copy-start | bytes 49156
  11.7 1.8 %copy-start.16 = (f32[32,128]{1,0:T(8,128)}, f32[32,128]{1,0:T(8,128)S(1)}, u32[]{:S(2)}) copy-start(f32[32,128]{1,0:T(8,128)S(1)} %collective-permute-done.3.refs_6_) | copy-start | bytes 49156
  17.0 4.4 %collective-permute-start.5 = (f32[224,128]{1,0:T(8,128)}, f32[224,128]{1,0:T(8,128)S(1)}, u32[]{:S(2)}, u32[]{:S(2)}) collective-permute-start(f32[224,128]{1,0:T(8,128)} %get-tuple-element.53), channel_id=1, source_target_pairs={{0,2},{2,4},{4,6},{6,0},{1,3},{3,5},{5,7},{7,1},{8,10},{10,12},{12... | collective-permute-start | bytes 344072 | tf_op jit(solution)/shard_map/ppermute | solution.py:67
  17.0 5.0 %collective-permute-start.6 = (f32[224,128]{1,0:T(8,128)}, f32[224,128]{1,0:T(8,128)S(1)}, u32[]{:S(2)}, u32[]{:S(2)}) collective-permute-start(f32[224,128]{1,0:T(8,128)} %get-tuple-element.54), channel_id=1, source_target_pairs={{0,6},{2,0},{4,2},{6,4},{1,7},{3,1},{5,3},{7,5},{8,14},{10,8},{12,... | collective-permute-start | bytes 344072 | tf_op jit(solution)/shard_map/ppermute | solution.py:67
  21.4 0.6 copy-start.9
  22.0 0.6 copy-start.11
  24.9 8.9 %collective-permute-start.7 = (f32[320,128]{1,0:T(8,128)}, f32[320,128]{1,0:T(8,128)S(1)}, u32[]{:S(2)}, u32[]{:S(2)}) collective-permute-start(f32[320,128]{1,0:T(8,128)} %get-tuple-element.58), channel_id=1, source_target_pairs={{0,8},{8,16},{16,24},{24,0},{1,9},{9,17},{17,25},{25,1},{2,10},{10... | collective-permute-start | bytes 491528 | tf_op jit(solution)/shard_map/ppermute | solution.py:67
  24.9 10.5 %collective-permute-start.8 = (f32[320,128]{1,0:T(8,128)}, f32[320,128]{1,0:T(8,128)S(1)}, u32[]{:S(2)}, u32[]{:S(2)}) collective-permute-start(f32[320,128]{1,0:T(8,128)} %get-tuple-element.59), channel_id=1, source_target_pairs={{0,24},{8,0},{16,8},{24,16},{1,25},{9,1},{17,9},{25,17},{2,26},{10... | collective-permute-start | bytes 491528 | tf_op jit(solution)/shard_map/ppermute | solution.py:67
  28.7 11.4 %all-to-all-start = ((f32[32,4,128]{2,1,0:T(4,128)}), f32[32,4,128]{2,1,0:T(4,128)S(1)}, u32[]{:S(2)}, u32[]{:S(2)}) async-start(f32[32,4,128]{2,1,0:T(4,128)} %bitcast.16), calls=%async_computation | async-start | bytes 131072 | tf_op jit(solution)/shard_map/all_to_all | solution.py:491
  33.8 1.6 %copy-start.4 = (f32[320,128]{1,0:T(8,128)}, f32[320,128]{1,0:T(8,128)S(1)}, u32[]{:S(2)}) copy-start(f32[320,128]{1,0:T(8,128)S(1)} %collective-permute-done.7.refs_3_) | copy-start | bytes 491524
  35.4 0.7 copy-start.6
  38.6 5.1 %collective-permute-start.9 = (f32[8,2560]{1,0:T(8,128)}, f32[8,2560]{1,0:T(8,128)S(1)}, u32[]{:S(2)}, u32[]{:S(2)}) collective-permute-start(f32[8,2560]{1,0:T(8,128)} %get-tuple-element.63), channel_id=1, source_target_pairs={{0,1},{1,0},{2,3},{3,2},{4,5},{5,4},{6,7},{7,6},{8,9},{9,8},{10,11... | collective-permute-start | bytes 245768 | tf_op jit(solution)/shard_map/ppermute | solution.py:67
  40.2 3.6 %copy-start.3 = (f32[32,4,128]{2,1,0:T(4,128)}, f32[32,4,128]{2,1,0:T(4,128)S(1)}, u32[]{:S(2)}) copy-start(f32[32,4,128]{2,1,0:T(4,128)S(1)} %all-to-all-done) | copy-start | bytes 196612
  43.8 0.6 copy-start.1
  55.3 4.5 %collective-permute-start.10 = (f32[224,128]{1,0:T(8,128)}, f32[224,128]{1,0:T(8,128)S(1)}, u32[]{:S(2)}, u32[]{:S(2)}) collective-permute-start(f32[224,128]{1,0:T(8,128)} %get-tuple-element.69), channel_id=1, source_target_pairs={{0,2},{2,4},{4,6},{6,0},{1,3},{3,5},{5,7},{7,1},{8,10},{10,12},{12... | collective-permute-start | bytes 344072 | tf_op jit(solution)/shard_map/ppermute | solution.py:67
  55.4 4.5 %collective-permute-start.11 = (f32[224,128]{1,0:T(8,128)}, f32[224,128]{1,0:T(8,128)S(1)}, u32[]{:S(2)}, u32[]{:S(2)}) collective-permute-start(f32[224,128]{1,0:T(8,128)} %get-tuple-element.70), channel_id=1, source_target_pairs={{0,6},{2,0},{4,2},{6,4},{1,7},{3,1},{5,3},{7,5},{8,14},{10,8},{12,... | collective-permute-start | bytes 344072 | tf_op jit(solution)/shard_map/ppermute | solution.py:67
  59.8 0.6 copy-start.10
  59.9 0.6 copy-start.12
  62.8 8.9 %collective-permute-start.12 = (f32[320,128]{1,0:T(8,128)}, f32[320,128]{1,0:T(8,128)S(1)}, u32[]{:S(2)}, u32[]{:S(2)}) collective-permute-start(f32[320,128]{1,0:T(8,128)} %get-tuple-element.74), channel_id=1, source_target_pairs={{0,8},{8,16},{16,24},{24,0},{1,9},{9,17},{17,25},{25,1},{2,10},{10... | collective-permute-start | bytes 491528 | tf_op jit(solution)/shard_map/ppermute | solution.py:67
  64.0 10.5 %collective-permute-start.13 = (f32[320,128]{1,0:T(8,128)}, f32[320,128]{1,0:T(8,128)S(1)}, u32[]{:S(2)}, u32[]{:S(2)}) collective-permute-start(f32[320,128]{1,0:T(8,128)} %get-tuple-element.75), channel_id=1, source_target_pairs={{0,24},{8,0},{16,8},{24,16},{1,25},{9,1},{17,9},{25,17},{2,26},{10... | collective-permute-start | bytes 491528 | tf_op jit(solution)/shard_map/ppermute | solution.py:67
  66.6 12.6 %all-to-all-start.1 = ((f32[32,4,128]{2,1,0:T(4,128)}), f32[32,4,128]{2,1,0:T(4,128)S(1)}, u32[]{:S(2)}, u32[]{:S(2)}) async-start(f32[32,4,128]{2,1,0:T(4,128)} %bitcast.15), calls=%async_computation.1 | async-start | bytes 131072 | tf_op jit(solution)/shard_map/all_to_all | solution.py:491
  71.7 2.8 %copy-start.5 = (f32[320,128]{1,0:T(8,128)}, f32[320,128]{1,0:T(8,128)S(1)}, u32[]{:S(2)}) copy-start(f32[320,128]{1,0:T(8,128)S(1)} %collective-permute-done.12.refs_3_) | copy-start | bytes 491524
  74.5 0.7 copy-start.7
  77.8 4.9 %collective-permute-start.14 = (f32[8,2560]{1,0:T(8,128)}, f32[8,2560]{1,0:T(8,128)S(1)}, u32[]{:S(2)}, u32[]{:S(2)}) collective-permute-start(f32[8,2560]{1,0:T(8,128)} %get-tuple-element.79), channel_id=1, source_target_pairs={{0,1},{1,0},{2,3},{3,2},{4,5},{5,4},{6,7},{7,6},{8,9},{9,8},{10,11... | collective-permute-start | bytes 245768 | tf_op jit(solution)/shard_map/ppermute | solution.py:67
  79.3 3.3 %copy-start = (f32[32,4,128]{2,1,0:T(4,128)}, f32[32,4,128]{2,1,0:T(4,128)S(1)}, u32[]{:S(2)}) copy-start(f32[32,4,128]{2,1,0:T(4,128)S(1)} %all-to-all-done.1) | copy-start | bytes 196612
  (2 other events, 1.2 us)

commit v3 on v2

--- a/solution.py
+++ b/solution.py
@@ -24,29 +24,31 @@
     return lax.dot_general(a, b, (dims, ((), ())), precision=HI, preferred_element_type=F32)
 
 
-def halves(x):
+def pieces_of(x):
     high = x.astype(jnp.bfloat16).astype(F32)
-    return high, x - high
+    rest = x - high
+    middle = rest.astype(jnp.bfloat16).astype(F32)
+    return high, middle, rest - middle
 
 
 def dot_right(x, hot):
-    both = jnp.concatenate(halves(x), axis=1).astype(jnp.bfloat16)
+    both = jnp.concatenate(pieces_of(x), axis=1).astype(jnp.bfloat16)
     return lax.dot_general(
-        both, jnp.concatenate([hot, hot], axis=0).astype(jnp.bfloat16), (((1,), (0,)), ((), ())), preferred_element_type=F32
+        both, jnp.concatenate([hot, hot, hot], axis=0).astype(jnp.bfloat16), (((1,), (0,)), ((), ())), preferred_element_type=F32
     )
 
 
 def dot_pick(hot, x):
-    both = jnp.concatenate(halves(x), axis=1).astype(jnp.bfloat16)
+    both = jnp.concatenate(pieces_of(x), axis=1).astype(jnp.bfloat16)
     return lax.dot_general(
-        jnp.concatenate([hot, hot], axis=1).astype(jnp.bfloat16), both, (((1,), (1,)), ((), ())), preferred_element_type=F32
+        jnp.concatenate([hot, hot, hot], axis=1).astype(jnp.bfloat16), both, (((1,), (1,)), ((), ())), preferred_element_type=F32
     )
 
 
 def dot_place(x, hot):
-    both = jnp.concatenate(halves(x), axis=0).astype(jnp.bfloat16)
+    both = jnp.concatenate(pieces_of(x), axis=0).astype(jnp.bfloat16)
     return lax.dot_general(
-        both, jnp.concatenate([hot, hot], axis=0).astype(jnp.bfloat16), (((0,), (0,)), ((), ())), preferred_element_type=F32
+        both, jnp.concatenate([hot, hot, hot], axis=0).astype(jnp.bfloat16), (((0,), (0,)), ((), ())), preferred_element_type=F32
     )
 
 

time: 109 us -> 110 us (level)
  Pallas kernels: 39.3 us -> 40.5 us
    pallas_call x9, Pallas kernels: 39.3 us -> 40.5 us  [call(): pl.pallas_call(body, out_shape=tuple(outs), in_specs=specs, out_specs=tup...]
  transfers between devices with their start and end apart: 17 -> 17, of which waited for: 12 -> 11; matrix products, arithmetic and copies ran while one was open for 1% -> 1% of each run, Pallas kernels for 5% -> 5%
where the time goes in v3:
time: 110 us
  Pallas kernels  40.5 us (37%)
  starting transfers between devices  28.5 us (26%)
  waiting for transfers between devices  23.6 us (21%)
  blocking collectives  11.5 us (10%)
  local copies, waits for them, and re-layouts  4.46 us (4%)
    pallas_call x9, Pallas kernels, call(): pl.pallas_call(body, out_shape=tuple(outs), in_specs=specs, out_specs=tup...  40.5 us
    ppermute x15, waiting for transfers between devices, cyclic(): lax.ppermute(value, axis, [(i, (i + by) % count) for i in range(count)])  23.6 us
    ppermute x15, starting transfers between devices, cyclic(): lax.ppermute(value, axis, [(i, (i + by) % count) for i in range(count)])  22.7 us
    all_to_all x1, blocking collectives, shards(): sums = lax.all_to_all(sums, AXES, 0, 0, tiled=True)  11.5 us
    all_to_all x2, starting transfers between devices, shards(): chunks = lax.all_to_all(chunk, AXES, 0, 0, tiled=True)  5.77 us
    unnamed x34, local copies, waits for them, and re-layouts  4.46 us
  transfers between devices with their start and end apart: 17, of which 11 were waited for; matrix products, arithmetic and copies ran while one was open for 1% of the time, Pallas kernels for 5%

profile of v3, /device:TPU:0, one launch (start us, length us, event | category | flops | bytes accessed | tf_op | source)
XLA Modules:
  0.0 110.0 jit_solution(13010525543544383935)
XLA Ops:
  0.6 2.0 %shard_map.41 = (f32[32,128]{1,0:T(8,128)}, f32[32,128]{1,0:T(8,128)}, f32[32,128]{1,0:T(8,128)}, f32[32,128]{1,0:T(8,128)}, f32[8,1024]{1,0:T(8,128)}) custom-call(f32[32,32,128]{2,1,0:T(8,128)} %refs_2_.3), custom_call_target="tpu_custom_call" | custom-call | tf_op jit(solution)/shard_map/pallas_call | solution.py:449
  2.6 3.1 %collective-permute-start = (f32[32,128]{1,0:T(8,128)}, f32[32,128]{1,0:T(8,128)S(1)}, u32[]{:S(2)}, u32[]{:S(2)}) collective-permute-start(f32[32,128]{1,0:T(8,128)} %get-tuple-element.45), channel_id=1, source_target_pairs={{0,8},{8,16},{16,24},{24,0},{1,9},{9,17},{17,25},{25,1},{2,10},{10... | collective-permute-start | bytes 49160 | tf_op jit(solution)/shard_map/ppermute | solution.py:69
  5.7 2.0 %collective-permute-start.1 = (f32[32,128]{1,0:T(8,128)}, f32[32,128]{1,0:T(8,128)S(1)}, u32[]{:S(2)}, u32[]{:S(2)}) collective-permute-start(f32[32,128]{1,0:T(8,128)} %get-tuple-element.46), channel_id=1, source_target_pairs={{0,24},{8,0},{16,8},{24,16},{1,25},{9,1},{17,9},{25,17},{2,26},{10... | collective-permute-start | bytes 49160 | tf_op jit(solution)/shard_map/ppermute | solution.py:69
  7.7 1.7 %collective-permute-start.3 = (f32[32,128]{1,0:T(8,128)}, f32[32,128]{1,0:T(8,128)S(1)}, u32[]{:S(2)}, u32[]{:S(2)}) collective-permute-start(f32[32,128]{1,0:T(8,128)} %get-tuple-element.48), channel_id=1, source_target_pairs={{0,6},{2,0},{4,2},{6,4},{1,7},{3,1},{5,3},{7,5},{8,14},{10,8},{12,... | collective-permute-start | bytes 49160 | tf_op jit(solution)/shard_map/ppermute | solution.py:69
  9.4 1.7 %collective-permute-start.4 = (f32[8,1024]{1,0:T(8,128)}, f32[8,1024]{1,0:T(8,128)S(1)}, u32[]{:S(2)}, u32[]{:S(2)}) collective-permute-start(f32[8,1024]{1,0:T(8,128)} %get-tuple-element.49), channel_id=1, source_target_pairs={{0,1},{1,0},{2,3},{3,2},{4,5},{5,4},{6,7},{7,6},{8,9},{9,8},{10,11... | collective-permute-start | bytes 98312 | tf_op jit(solution)/shard_map/ppermute | solution.py:69
  11.8 1.8 %collective-permute-done.4.refs_7_.refs_8_ = f32[8,1024]{1,0:T(8,128)S(1)} collective-permute-done((f32[8,1024]{1,0:T(8,128)}, f32[8,1024]{1,0:T(8,128)S(1)}, u32[]{:S(2)}, u32[]{:S(2)}) %collective-permute-start.4) | collective-permute-done | bytes 32800 | tf_op jit(solution)/shard_map/ppermute | solution.py:69
  14.2 3.0 %shard_map.42 = (f32[32,32,128]{2,1,0:T(8,128)}, f32[16,16,128]{2,1,0:T(8,128)}, f32[8,8,128]{2,1,0:T(8,128)}, f32[224,128]{1,0:T(8,128)}, f32[224,128]{1,0:T(8,128)}, /*index=5*/f32[128,128]{1,0:T(8,128)}) custom-call(s32[3]{0:T(128)} %pad_add_fusion.refs_0_, f32[32,32,128]{2,1,0:T(8,128)} %refs_1_.1, f32[32,32,128]{2,1,0:T(8,128)} %refs_2_.3, ...), custom_call_target="tpu_custom_call" | custom-call | tf_op jit(solution)/shard_map/pallas_call | solution.py:449
  17.2 1.7 %collective-permute-start.6 = (f32[224,128]{1,0:T(8,128)}, f32[224,128]{1,0:T(8,128)S(1)}, u32[]{:S(2)}, u32[]{:S(2)}) collective-permute-start(f32[224,128]{1,0:T(8,128)} %get-tuple-element.54), channel_id=1, source_target_pairs={{0,6},{2,0},{4,2},{6,4},{1,7},{3,1},{5,3},{7,5},{8,14},{10,8},{12,... | collective-permute-start | bytes 344072 | tf_op jit(solution)/shard_map/ppermute | solution.py:69
  18.9 2.7 %collective-permute-done.5.refs_3_ = f32[224,128]{1,0:T(8,128)S(1)} collective-permute-done((f32[224,128]{1,0:T(8,128)}, f32[224,128]{1,0:T(8,128)S(1)}, u32[]{:S(2)}, u32[]{:S(2)}) %collective-permute-start.5) | collective-permute-done | bytes 114720 | tf_op jit(solution)/shard_map/ppermute | solution.py:69
  22.8 2.2 %shard_map.43 = (f32[32,40,128]{2,1,0:T(8,128)}, f32[16,24,128]{2,1,0:T(8,128)}, f32[8,16,128]{2,1,0:T(8,128)}, f32[320,128]{1,0:T(8,128)}, f32[320,128]{1,0:T(8,128)}) custom-call(f32[32,32,128]{2,1,0:T(8,128)} %get-tuple-element.50.refs_0_.refs_3_, f32[16,16,128]{2,1,0:T(8,128)} %get-tuple-element.51.refs_1_, f32[8,8,128]{2,1,0:T(8,128)} %get-tuple-element.52.refs_2_, ...), custom_call_target="tpu_custom_call" | custom-call | tf_op jit(solution)/shard_map/pallas_call | solution.py:449
  25.1 3.8 %collective-permute-start.8 = (f32[320,128]{1,0:T(8,128)}, f32[320,128]{1,0:T(8,128)S(1)}, u32[]{:S(2)}, u32[]{:S(2)}) collective-permute-start(f32[320,128]{1,0:T(8,128)} %get-tuple-element.59), channel_id=1, source_target_pairs={{0,24},{8,0},{16,8},{24,16},{1,25},{9,1},{17,9},{25,17},{2,26},{10... | collective-permute-start | bytes 491528 | tf_op jit(solution)/shard_map/ppermute | solution.py:69
  28.9 2.9 %all-to-all-start = ((f32[32,4,128]{2,1,0:T(4,128)}), f32[32,4,128]{2,1,0:T(4,128)S(1)}, u32[]{:S(2)}, u32[]{:S(2)}) async-start(f32[32,4,128]{2,1,0:T(4,128)} %bitcast.16), calls=%async_computation | async-start | bytes 131072 | tf_op jit(solution)/shard_map/all_to_all | solution.py:493
  31.8 2.1 %collective-permute-done.7.refs_3_ = f32[320,128]{1,0:T(8,128)S(1)} collective-permute-done((f32[320,128]{1,0:T(8,128)}, f32[320,128]{1,0:T(8,128)S(1)}, u32[]{:S(2)}, u32[]{:S(2)}) %collective-permute-start.7) | collective-permute-done | bytes 163872 | tf_op jit(solution)/shard_map/ppermute | solution.py:69
  34.0 1.6 %collective-permute-done.8.refs_4_ = f32[320,128]{1,0:T(8,128)S(1)} collective-permute-done((f32[320,128]{1,0:T(8,128)}, f32[320,128]{1,0:T(8,128)S(1)}, u32[]{:S(2)}, u32[]{:S(2)}) %collective-permute-start.8) | collective-permute-done | bytes 163872 | tf_op jit(solution)/shard_map/ppermute | solution.py:69
  36.2 2.6 %shard_map.44 = (f32[40,40,128]{2,1,0:T(8,128)}, f32[24,24,128]{2,1,0:T(8,128)}, f32[16,16,128]{2,1,0:T(8,128)}, f32[8,2560]{1,0:T(8,128)}) custom-call(f32[32,40,128]{2,1,0:T(8,128)} %get-tuple-element.55.refs_0_, f32[16,24,128]{2,1,0:T(8,128)} %get-tuple-element.56.refs_1_, f32[8,16,128]{2,1,0:T(8,128)} %get-tuple-element.57.refs_2_, ...), custom_call_target="tpu_custom_call" | custom-call | tf_op jit(solution)/shard_map/pallas_call | solution.py:449
  38.9 1.5 %collective-permute-start.9 = (f32[8,2560]{1,0:T(8,128)}, f32[8,2560]{1,0:T(8,128)S(1)}, u32[]{:S(2)}, u32[]{:S(2)}) collective-permute-start(f32[8,2560]{1,0:T(8,128)} %get-tuple-element.63), channel_id=1, source_target_pairs={{0,1},{1,0},{2,3},{3,2},{4,5},{5,4},{6,7},{7,6},{8,9},{9,8},{10,11... | collective-permute-start | bytes 245768 | tf_op jit(solution)/shard_map/ppermute | solution.py:69
  40.4 3.7 %collective-permute-done.9.refs_4_.refs_5_ = f32[8,2560]{1,0:T(8,128)S(1)} collective-permute-done((f32[8,2560]{1,0:T(8,128)}, f32[8,2560]{1,0:T(8,128)S(1)}, u32[]{:S(2)}, u32[]{:S(2)}) %collective-permute-start.9) | collective-permute-done | bytes 81952 | tf_op jit(solution)/shard_map/ppermute | solution.py:69
  44.6 11.3 %shard_map.45 = (f32[32,32,128]{2,1,0:T(8,128)}, f32[32,32,128]{2,1,0:T(8,128)}, f32[16,16,128]{2,1,0:T(8,128)}, f32[8,8,128]{2,1,0:T(8,128)}, f32[224,128]{1,0:...) custom-call(s32[3]{0:T(128)} %pad_add_fusion.refs_0_, ...), custom_call_target="tpu_custom_call" | custom-call | tf_op jit(solution)/shard_map/pallas_call | solution.py:449
  56.0 1.7 %collective-permute-start.11 = (f32[224,128]{1,0:T(8,128)}, f32[224,128]{1,0:T(8,128)S(1)}, u32[]{:S(2)}, u32[]{:S(2)}) collective-permute-start(f32[224,128]{1,0:T(8,128)} %get-tuple-element.70), channel_id=1, source_target_pairs={{0,6},{2,0},{4,2},{6,4},{1,7},{3,1},{5,3},{7,5},{8,14},{10,8},{12,... | collective-permute-start | bytes 344072 | tf_op jit(solution)/shard_map/ppermute | solution.py:69
  57.8 2.7 %collective-permute-done.10.refs_3_ = f32[224,128]{1,0:T(8,128)S(1)} collective-permute-done((f32[224,128]{1,0:T(8,128)}, f32[224,128]{1,0:T(8,128)S(1)}, u32[]{:S(2)}, u32[]{:S(2)}) %collective-permute-start.10) | collective-permute-done | bytes 114720 | tf_op jit(solution)/shard_map/ppermute | solution.py:69
  61.2 2.2 %shard_map.46 = (f32[32,40,128]{2,1,0:T(8,128)}, f32[16,24,128]{2,1,0:T(8,128)}, f32[8,16,128]{2,1,0:T(8,128)}, f32[320,128]{1,0:T(8,128)}, f32[320,128]{1,0:T(8,128)}) custom-call(f32[32,32,128]{2,1,0:T(8,128)} %get-tuple-element.66.refs_0_.refs_5_, f32[16,16,128]{2,1,0:T(8,128)} %get-tuple-element.67.refs_1_, f32[8,8,128]{2,1,0:T(8,128)} %get-tuple-element.68.refs_2_, ...), custom_call_target="tpu_custom_call" | custom-call | tf_op jit(solution)/shard_map/pallas_call | solution.py:449
  63.5 1.2 %collective-permute-start.12 = (f32[320,128]{1,0:T(8,128)}, f32[320,128]{1,0:T(8,128)S(1)}, u32[]{:S(2)}, u32[]{:S(2)}) collective-permute-start(f32[320,128]{1,0:T(8,128)} %get-tuple-element.74), channel_id=1, source_target_pairs={{0,8},{8,16},{16,24},{24,0},{1,9},{9,17},{17,25},{25,1},{2,10},{10... | collective-permute-start | bytes 491528 | tf_op jit(solution)/shard_map/ppermute | solution.py:69
  64.6 2.7 %collective-permute-start.13 = (f32[320,128]{1,0:T(8,128)}, f32[320,128]{1,0:T(8,128)S(1)}, u32[]{:S(2)}, u32[]{:S(2)}) collective-permute-start(f32[320,128]{1,0:T(8,128)} %get-tuple-element.75), channel_id=1, source_target_pairs={{0,24},{8,0},{16,8},{24,16},{1,25},{9,1},{17,9},{25,17},{2,26},{10... | collective-permute-start | bytes 491528 | tf_op jit(solution)/shard_map/ppermute | solution.py:69
  67.3 2.9 %all-to-all-start.1 = ((f32[32,4,128]{2,1,0:T(4,128)}), f32[32,4,128]{2,1,0:T(4,128)S(1)}, u32[]{:S(2)}, u32[]{:S(2)}) async-start(f32[32,4,128]{2,1,0:T(4,128)} %bitcast.15), calls=%async_computation.1 | async-start | bytes 131072 | tf_op jit(solution)/shard_map/all_to_all | solution.py:493
  70.2 2.2 %collective-permute-done.12.refs_3_ = f32[320,128]{1,0:T(8,128)S(1)} collective-permute-done((f32[320,128]{1,0:T(8,128)}, f32[320,128]{1,0:T(8,128)S(1)}, u32[]{:S(2)}, u32[]{:S(2)}) %collective-permute-start.12) | collective-permute-done | bytes 163872 | tf_op jit(solution)/shard_map/ppermute | solution.py:69
  72.4 2.8 %collective-permute-done.13.refs_4_ = f32[320,128]{1,0:T(8,128)S(1)} collective-permute-done((f32[320,128]{1,0:T(8,128)}, f32[320,128]{1,0:T(8,128)S(1)}, u32[]{:S(2)}, u32[]{:S(2)}) %collective-permute-start.13) | collective-permute-done | bytes 163872 | tf_op jit(solution)/shard_map/ppermute | solution.py:69
  75.8 2.6 %shard_map.47 = (f32[40,40,128]{2,1,0:T(8,128)}, f32[24,24,128]{2,1,0:T(8,128)}, f32[16,16,128]{2,1,0:T(8,128)}, f32[8,2560]{1,0:T(8,128)}) custom-call(f32[32,40,128]{2,1,0:T(8,128)} %get-tuple-element.71.refs_0_, f32[16,24,128]{2,1,0:T(8,128)} %get-tuple-element.72.refs_1_, f32[8,16,128]{2,1,0:T(8,128)} %get-tuple-element.73.refs_2_, ...), custom_call_target="tpu_custom_call" | custom-call | tf_op jit(solution)/shard_map/pallas_call | solution.py:449
  78.5 1.5 %collective-permute-start.14 = (f32[8,2560]{1,0:T(8,128)}, f32[8,2560]{1,0:T(8,128)S(1)}, u32[]{:S(2)}, u32[]{:S(2)}) collective-permute-start(f32[8,2560]{1,0:T(8,128)} %get-tuple-element.79), channel_id=1, source_target_pairs={{0,1},{1,0},{2,3},{3,2},{4,5},{5,4},{6,7},{7,6},{8,9},{9,8},{10,11... | collective-permute-start | bytes 245768 | tf_op jit(solution)/shard_map/ppermute | solution.py:69
  80.0 3.3 %collective-permute-done.14.refs_4_.refs_5_ = f32[8,2560]{1,0:T(8,128)S(1)} collective-permute-done((f32[8,2560]{1,0:T(8,128)}, f32[8,2560]{1,0:T(8,128)S(1)}, u32[]{:S(2)}, u32[]{:S(2)}) %collective-permute-start.14) | collective-permute-done | bytes 81952 | tf_op jit(solution)/shard_map/ppermute | solution.py:69
  84.0 11.3 %shard_map.48 = (f32[32,32,128]{2,1,0:T(8,128)}, f32[32,32,128]{2,1,0:T(8,128)}, f32[32,128]{1,0:T(8,128)}) custom-call(s32[3]{0:T(128)} %pad_add_fusion.refs_0_, f32[40,40,128]{2,1,0:T(8,128)} %get-tuple-element.76.refs_1_, f32[24,24,128]{2,1,0:T(8,128)} %get-tuple-element.77.refs_2_, f32[16,16,128]{2,1,0:T(8,128)} %get-tuple-element.78.refs_3_, ...), custom_call_target="tpu_custom_call" | custom-call | tf_op jit(solution)/shard_map/pallas_call | solution.py:449
  95.3 11.5 %all_to_all.33 = f32[32,1,128]{2,1,0:T(1,128)} all-to-all(f32[32,1,128]{2,1,0:T(1,128)} %bitcast.17), channel_id=1, replica_groups=mesh['gx'=4,'gy'=4,'gz'=2] {'gx','gy','gz'}, dimensions={0} | all-to-all | bytes 32768 | tf_op jit(solution)/shard_map/all_to_all | solution.py:518
  106.8 3.2 %shard_map.49 = (f32[32,32,128]{2,1,0:T(8,128)}, f32[32,32,128]{2,1,0:T(8,128)}) custom-call(f32[128,128]{1,0:T(8,128)} %bitcast.12, f32[32,128]{1,0:T(8,128)} %bitcast.14, f32[32,32,128]{2,1,0:T(8,128)} %refs_2_.3, f32[32,32,128]{2,1,0:T(8,128)} %get-tuple-element.50.refs_0_.refs_3_, f32[32,32,128]{2,1,0:T(8,128)} %get-tuple-element.85.refs_4_, ...), custom_call_target="tpu_custom_call" | custom-call | tf_op jit(solution)/shard_map/pallas_call | solution.py:449
  (47 shorter events, 5.9 us)
Async XLA Ops:
  2.6 9.1 %collective-permute-start = (f32[32,128]{1,0:T(8,128)}, f32[32,128]{1,0:T(8,128)S(1)}, u32[]{:S(2)}, u32[]{:S(2)}) collective-permute-start(f32[32,128]{1,0:T(8,128)} %get-tuple-element.45), channel_id=1, source_target_pairs={{0,8},{8,16},{16,24},{24,0},{1,9},{9,17},{17,25},{25,1},{2,10},{10... | collective-permute-start | bytes 49160 | tf_op jit(solution)/shard_map/ppermute | solution.py:69
  5.7 6.1 %collective-permute-start.1 = (f32[32,128]{1,0:T(8,128)}, f32[32,128]{1,0:T(8,128)S(1)}, u32[]{:S(2)}, u32[]{:S(2)}) collective-permute-start(f32[32,128]{1,0:T(8,128)} %get-tuple-element.46), channel_id=1, source_target_pairs={{0,24},{8,0},{16,8},{24,16},{1,25},{9,1},{17,9},{25,17},{2,26},{10... | collective-permute-start | bytes 49160 | tf_op jit(solution)/shard_map/ppermute | solution.py:69
  7.7 4.1 %collective-permute-start.2 = (f32[32,128]{1,0:T(8,128)}, f32[32,128]{1,0:T(8,128)S(1)}, u32[]{:S(2)}, u32[]{:S(2)}) collective-permute-start(f32[32,128]{1,0:T(8,128)} %get-tuple-element.47), channel_id=1, source_target_pairs={{0,2},{2,4},{4,6},{6,0},{1,3},{3,5},{5,7},{7,1},{8,10},{10,12},{12... | collective-permute-start | bytes 49160 | tf_op jit(solution)/shard_map/ppermute | solution.py:69
  7.7 4.1 %collective-permute-start.3 = (f32[32,128]{1,0:T(8,128)}, f32[32,128]{1,0:T(8,128)S(1)}, u32[]{:S(2)}, u32[]{:S(2)}) collective-permute-start(f32[32,128]{1,0:T(8,128)} %get-tuple-element.48), channel_id=1, source_target_pairs={{0,6},{2,0},{4,2},{6,4},{1,7},{3,1},{5,3},{7,5},{8,14},{10,8},{12,... | collective-permute-start | bytes 49160 | tf_op jit(solution)/shard_map/ppermute | solution.py:69
  9.4 4.1 %collective-permute-start.4 = (f32[8,1024]{1,0:T(8,128)}, f32[8,1024]{1,0:T(8,128)S(1)}, u32[]{:S(2)}, u32[]{:S(2)}) collective-permute-start(f32[8,1024]{1,0:T(8,128)} %get-tuple-element.49), channel_id=1, source_target_pairs={{0,1},{1,0},{2,3},{3,2},{4,5},{5,4},{6,7},{7,6},{8,9},{9,8},{10,11... | collective-permute-start | bytes 98312 | tf_op jit(solution)/shard_map/ppermute | solution.py:69
  11.8 1.8 %copy-start.13 = (f32[32,128]{1,0:T(8,128)}, f32[32,128]{1,0:T(8,128)S(1)}, u32[]{:S(2)}) copy-start(f32[32,128]{1,0:T(8,128)S(1)} %collective-permute-done.refs_3_) | copy-start | bytes 49156
  11.8 1.8 %copy-start.14 = (f32[32,128]{1,0:T(8,128)}, f32[32,128]{1,0:T(8,128)S(1)}, u32[]{:S(2)}) copy-start(f32[32,128]{1,0:T(8,128)S(1)} %collective-permute-done.1.refs_4_) | copy-start | bytes 49156
  11.8 1.8 %copy-start.15 = (f32[32,128]{1,0:T(8,128)}, f32[32,128]{1,0:T(8,128)S(1)}, u32[]{:S(2)}) copy-start(f32[32,128]{1,0:T(8,128)S(1)} %collective-permute-done.2.refs_5_) | copy-start | bytes 49156
  11.8 1.8 %copy-start.16 = (f32[32,128]{1,0:T(8,128)}, f32[32,128]{1,0:T(8,128)S(1)}, u32[]{:S(2)}) copy-start(f32[32,128]{1,0:T(8,128)S(1)} %collective-permute-done.3.refs_6_) | copy-start | bytes 49156
  17.2 4.4 %collective-permute-start.5 = (f32[224,128]{1,0:T(8,128)}, f32[224,128]{1,0:T(8,128)S(1)}, u32[]{:S(2)}, u32[]{:S(2)}) collective-permute-start(f32[224,128]{1,0:T(8,128)} %get-tuple-element.53), channel_id=1, source_target_pairs={{0,2},{2,4},{4,6},{6,0},{1,3},{3,5},{5,7},{7,1},{8,10},{10,12},{12... | collective-permute-start | bytes 344072 | tf_op jit(solution)/shard_map/ppermute | solution.py:69
  17.2 5.0 %collective-permute-start.6 = (f32[224,128]{1,0:T(8,128)}, f32[224,128]{1,0:T(8,128)S(1)}, u32[]{:S(2)}, u32[]{:S(2)}) collective-permute-start(f32[224,128]{1,0:T(8,128)} %get-tuple-element.54), channel_id=1, source_target_pairs={{0,6},{2,0},{4,2},{6,4},{1,7},{3,1},{5,3},{7,5},{8,14},{10,8},{12,... | collective-permute-start | bytes 344072 | tf_op jit(solution)/shard_map/ppermute | solution.py:69
  21.6 0.6 copy-start.9
  22.2 0.6 copy-start.11
  25.1 8.9 %collective-permute-start.7 = (f32[320,128]{1,0:T(8,128)}, f32[320,128]{1,0:T(8,128)S(1)}, u32[]{:S(2)}, u32[]{:S(2)}) collective-permute-start(f32[320,128]{1,0:T(8,128)} %get-tuple-element.58), channel_id=1, source_target_pairs={{0,8},{8,16},{16,24},{24,0},{1,9},{9,17},{17,25},{25,1},{2,10},{10... | collective-permute-start | bytes 491528 | tf_op jit(solution)/shard_map/ppermute | solution.py:69
  25.1 10.5 %collective-permute-start.8 = (f32[320,128]{1,0:T(8,128)}, f32[320,128]{1,0:T(8,128)S(1)}, u32[]{:S(2)}, u32[]{:S(2)}) collective-permute-start(f32[320,128]{1,0:T(8,128)} %get-tuple-element.59), channel_id=1, source_target_pairs={{0,24},{8,0},{16,8},{24,16},{1,25},{9,1},{17,9},{25,17},{2,26},{10... | collective-permute-start | bytes 491528 | tf_op jit(solution)/shard_map/ppermute | solution.py:69
  28.9 11.5 %all-to-all-start = ((f32[32,4,128]{2,1,0:T(4,128)}), f32[32,4,128]{2,1,0:T(4,128)S(1)}, u32[]{:S(2)}, u32[]{:S(2)}) async-start(f32[32,4,128]{2,1,0:T(4,128)} %bitcast.16), calls=%async_computation | async-start | bytes 131072 | tf_op jit(solution)/shard_map/all_to_all | solution.py:493
  34.0 1.6 %copy-start.4 = (f32[320,128]{1,0:T(8,128)}, f32[320,128]{1,0:T(8,128)S(1)}, u32[]{:S(2)}) copy-start(f32[320,128]{1,0:T(8,128)S(1)} %collective-permute-done.7.refs_3_) | copy-start | bytes 491524
  35.6 0.7 copy-start.6
  38.9 5.1 %collective-permute-start.9 = (f32[8,2560]{1,0:T(8,128)}, f32[8,2560]{1,0:T(8,128)S(1)}, u32[]{:S(2)}, u32[]{:S(2)}) collective-permute-start(f32[8,2560]{1,0:T(8,128)} %get-tuple-element.63), channel_id=1, source_target_pairs={{0,1},{1,0},{2,3},{3,2},{4,5},{5,4},{6,7},{7,6},{8,9},{9,8},{10,11... | collective-permute-start | bytes 245768 | tf_op jit(solution)/shard_map/ppermute | solution.py:69
  40.4 3.7 %copy-start.3 = (f32[32,4,128]{2,1,0:T(4,128)}, f32[32,4,128]{2,1,0:T(4,128)S(1)}, u32[]{:S(2)}) copy-start(f32[32,4,128]{2,1,0:T(4,128)S(1)} %all-to-all-done) | copy-start | bytes 196612
  44.0 0.6 copy-start.1
  56.0 4.5 %collective-permute-start.10 = (f32[224,128]{1,0:T(8,128)}, f32[224,128]{1,0:T(8,128)S(1)}, u32[]{:S(2)}, u32[]{:S(2)}) collective-permute-start(f32[224,128]{1,0:T(8,128)} %get-tuple-element.69), channel_id=1, source_target_pairs={{0,2},{2,4},{4,6},{6,0},{1,3},{3,5},{5,7},{7,1},{8,10},{10,12},{12... | collective-permute-start | bytes 344072 | tf_op jit(solution)/shard_map/ppermute | solution.py:69
  56.0 4.6 %collective-permute-start.11 = (f32[224,128]{1,0:T(8,128)}, f32[224,128]{1,0:T(8,128)S(1)}, u32[]{:S(2)}, u32[]{:S(2)}) collective-permute-start(f32[224,128]{1,0:T(8,128)} %get-tuple-element.70), channel_id=1, source_target_pairs={{0,6},{2,0},{4,2},{6,4},{1,7},{3,1},{5,3},{7,5},{8,14},{10,8},{12,... | collective-permute-start | bytes 344072 | tf_op jit(solution)/shard_map/ppermute | solution.py:69
  60.5 0.6 copy-start.10
  60.6 0.6 copy-start.12
  63.5 8.9 %collective-permute-start.12 = (f32[320,128]{1,0:T(8,128)}, f32[320,128]{1,0:T(8,128)S(1)}, u32[]{:S(2)}, u32[]{:S(2)}) collective-permute-start(f32[320,128]{1,0:T(8,128)} %get-tuple-element.74), channel_id=1, source_target_pairs={{0,8},{8,16},{16,24},{24,0},{1,9},{9,17},{17,25},{25,1},{2,10},{10... | collective-permute-start | bytes 491528 | tf_op jit(solution)/shard_map/ppermute | solution.py:69
  64.6 10.6 %collective-permute-start.13 = (f32[320,128]{1,0:T(8,128)}, f32[320,128]{1,0:T(8,128)S(1)}, u32[]{:S(2)}, u32[]{:S(2)}) collective-permute-start(f32[320,128]{1,0:T(8,128)} %get-tuple-element.75), channel_id=1, source_target_pairs={{0,24},{8,0},{16,8},{24,16},{1,25},{9,1},{17,9},{25,17},{2,26},{10... | collective-permute-start | bytes 491528 | tf_op jit(solution)/shard_map/ppermute | solution.py:69
  67.3 12.7 %all-to-all-start.1 = ((f32[32,4,128]{2,1,0:T(4,128)}), f32[32,4,128]{2,1,0:T(4,128)S(1)}, u32[]{:S(2)}, u32[]{:S(2)}) async-start(f32[32,4,128]{2,1,0:T(4,128)} %bitcast.15), calls=%async_computation.1 | async-start | bytes 131072 | tf_op jit(solution)/shard_map/all_to_all | solution.py:493
  72.4 2.8 %copy-start.5 = (f32[320,128]{1,0:T(8,128)}, f32[320,128]{1,0:T(8,128)S(1)}, u32[]{:S(2)}) copy-start(f32[320,128]{1,0:T(8,128)S(1)} %collective-permute-done.12.refs_3_) | copy-start | bytes 491524
  75.2 0.7 copy-start.7
  78.5 4.9 %collective-permute-start.14 = (f32[8,2560]{1,0:T(8,128)}, f32[8,2560]{1,0:T(8,128)S(1)}, u32[]{:S(2)}, u32[]{:S(2)}) collective-permute-start(f32[8,2560]{1,0:T(8,128)} %get-tuple-element.79), channel_id=1, source_target_pairs={{0,1},{1,0},{2,3},{3,2},{4,5},{5,4},{6,7},{7,6},{8,9},{9,8},{10,11... | collective-permute-start | bytes 245768 | tf_op jit(solution)/shard_map/ppermute | solution.py:69
  80.0 3.3 %copy-start = (f32[32,4,128]{2,1,0:T(4,128)}, f32[32,4,128]{2,1,0:T(4,128)S(1)}, u32[]{:S(2)}) copy-start(f32[32,4,128]{2,1,0:T(4,128)S(1)} %all-to-all-done.1) | copy-start | bytes 196612
  (2 other events, 1.2 us)
